TPU v7x, 32 devices: a whole 2x2x4 slice. The times are simulated.
32 devices in a mesh: gx: 4 (over z), yz: 8 (over y, x, core).
Axes of the slice: x: 2, y: 2, z: 4, core: 2. Of those that a mesh axis runs over, the one named last changes fastest.
Arguments:
- positions: bfloat16 [3, 8192], P(None, ('gx', 'yz')), may hold values from 0 to 1
- species: int32 [8192], P(('gx', 'yz')), may hold values from 0 to 5
- features: bfloat16 [8192, 512], P(('gx', 'yz')), may hold values from -6 to 6
- move_dest: int32 [64], P(('gx', 'yz')), may hold values from 0 to 7, as said below
- move_slot: int32 [64], P(('gx', 'yz')), may hold values from 0 to 1, as said below
- halo_list: int32 [1024], P(('gx', 'yz')), may hold values from 0 to 255
- neighbours: int32 [8192, 64], P(('gx', 'yz')), may hold values from 0 to 383, as said below
- neighbour_count: int32 [8192], P(('gx', 'yz')), may hold values from 16 to 64
- wave_index: int32 [3, 4096], replicated, may hold values from -16 to 16, as said below
- radial_in: bfloat16 [8, 64], replicated, may hold values from -2 to 2
- radial_mid: bfloat16 [2, 64, 64], replicated, may hold values from -0.75 to 0.75
- radial_out: bfloat16 [64, 512], replicated, may hold values from -0.75 to 0.75
- up_weight: bfloat16 [2, 128, 128], replicated, may hold values from -0.5 to 0.5
- prod_weight: float32 [6, 640], replicated, may hold values from -4 to 4
- out_weight: bfloat16 [2, 128, 128], replicated, may hold values from -0.5 to 0.5
- skip_weight: bfloat16 [2, 128, 128], replicated, may hold values from -0.5 to 0.5
- charge_weight: bfloat16 [128, 8], replicated, may hold values from -0.5 to 0.5
- field_weight: float32 [8, 128], replicated, may hold values from -2 to 2
- read_weight: bfloat16 [128, 16], replicated, may hold values from -0.5 to 0.5
- read_vector: float32 [16], replicated, may hold values from -1.5 to 1.5
- force_weight: float32 [128], replicated, may hold values from -0.5 to 0.5
Outputs:
- forces: float32 [3, 8192], P(None, ('gx', 'yz'))
- energies: float32 [8192], P(('gx', 'yz'))
Inputs may be any that keep to these rules, and one draw needn't show every extreme that they name: `move_dest`: the destination lies in the same gx row. Exactly 2 blocks of each device go to other devices, at most one to any one device, and each device receives exactly 2 blocks; the others stay. `move_slot`: the 2 blocks that a device holds after the move take its 2 slots once each. `neighbours`: row of the device's table: its working atoms, then the ghosts from gx - 1, gx + 1, yz - 1, yz + 1. Never the atom itself; slots from neighbour_count on are padding. `wave_index`: row 0 runs from 1 to 8, row 1 from -16 to 16, row 2 from -2 to 2.
All inputs are finite; a program needn't handle non-finite values.
Results may differ from a plain program's by a relative error of at most 0.0028.
Values may be sent and summed in bfloat16 or wider, within the bound.
A program may use at most 64 MiB of HBM per device.

v0:
```python
import functools
import math

import jax
import jax.numpy as jnp
from jax import lax
from jax.experimental import pallas as pl
from jax.experimental.pallas import tpu as pltpu
from jax.sharding import PartitionSpec as P

highest = lax.Precision.HIGHEST
two_pi = 2.0 * math.pi
cutoff_radius = 3.5
basis_sharpness = 4.0
ewald_width = 0.1
ewald_scale = 0.01
z_reach = 2
lanes = 128
f32 = jnp.float32
bf16 = jnp.bfloat16

VMEM = pl.BlockSpec(memory_space=pltpu.VMEM)
SMEM = pl.BlockSpec(memory_space=pltpu.SMEM)
NT = (((1,), (1,)), ((), ()))
TN = (((0,), (0,)), ((), ()))


def nt(a, b, precision=None):
    return lax.dot_general(a, b, NT, precision=precision, preferred_element_type=f32)


def tn(a, b, precision=None):
    return lax.dot_general(a, b, TN, precision=precision, preferred_element_type=f32)


def mm(a, b, precision=None):
    return jnp.dot(a, b, precision=precision, preferred_element_type=f32)


def iota(shape, dim):
    return lax.broadcasted_iota(jnp.int32, shape, dim)


def silu(v):
    half = 0.5 * v
    return half + half * jnp.tanh(half)


def turn_cos_sin(turns):
    frac = turns - jnp.floor(turns + 0.5)
    angle = two_pi * frac
    return jnp.cos(angle), jnp.sin(angle)


def send_kernel(dest, slot, feat, pos, species, out):
    peers, block, _ = out.shape
    atoms, width = feat.shape
    blocks = atoms // block
    rows = jnp.concatenate(
        [pos[...].astype(f32), species[...].astype(f32), jnp.zeros((lanes - 4, atoms), f32)], axis=0
    )
    cols = rows.T
    lane = iota((block, lanes), 1)
    for d in range(peers):
        total = jnp.zeros((block, width), f32)
        side = jnp.zeros((block, lanes), f32)
        for b in range(blocks):
            chosen = jnp.where(dest[b] == d, 1.0, 0.0).astype(f32)
            total = total + chosen * feat[b * block : (b + 1) * block, :].astype(f32)
            mark = (slot[b] + 1).astype(f32)
            part = jnp.where(lane == 4, mark, cols[b * block : (b + 1) * block, :])
            side = side + chosen * part
        out[d, :, :width] = total.astype(bf16)
        out[d, :, width:] = side.astype(bf16)


def arrive_kernel(recv, halo, work, send, codes):
    peers, block, full = recv.shape
    atoms = work.shape[0]
    blocks = atoms // block
    width = full - lanes
    for s in range(blocks):
        total = jnp.zeros((block, full), f32)
        for d in range(peers):
            mark = recv[d, :, width + 4 : width + 5].astype(f32)
            total = total + jnp.where(mark == s + 1.0, 1.0, 0.0) * recv[d].astype(f32)
        work[s * block : (s + 1) * block, :] = total.astype(bf16)
    for d in range(peers):
        codes[d : d + 1, :] = jnp.broadcast_to(
            recv[d, 0:1, width + 4 : width + 5].astype(f32), (1, lanes)
        )
    count = halo.shape[0]
    pick = (halo[...] == iota((count, atoms), 1)).astype(f32).astype(bf16)
    send[...] = mm(pick, work[...]).astype(bf16)


def xz_factors(x_turns, z_turns, nx):
    steps = (iota((nx, x_turns.shape[1]), 0) + 1).astype(f32)
    xc, xs = turn_cos_sin(steps * x_turns)
    cos_rows, sin_rows = [], []
    for m in range(-z_reach, z_reach + 1):
        zc, zs = turn_cos_sin(m * z_turns)
        cos_rows.append(xc * zc - xs * zs)
        sin_rows.append(xc * zs + xs * zc)
    return jnp.concatenate(cos_rows, axis=0), jnp.concatenate(sin_rows, axis=0)


def wave_kernel(gx, yz, nyp, place, work, charge_t, partial, phases, charges):
    atoms, full = work.shape
    channels = charge_t.shape[1]
    pos = work[:, full - lanes :].astype(f32).T
    x_turns = (pos[0:1] + place[0]) * (1.0 / gx)
    y_turns = (pos[1:2] + place[1]) * (1.0 / yz)
    nx = 2 * gx
    xzc, xzs = xz_factors(x_turns, pos[2:3], nx)
    yc, ys = turn_cos_sin(iota((nyp, atoms), 0).astype(f32) * y_turns)
    q = nt(charge_t[...], work[:, :channels])
    pairs, latent = xzc.shape[0], q.shape[0]
    real = (xzc[:, None, :] * q[None]).reshape(pairs * latent, atoms)
    imag = (xzs[:, None, :] * q[None]).reshape(pairs * latent, atoms)
    ycs = jnp.concatenate([yc, ys], axis=0)
    partial[: 2 * nyp, :] = nt(ycs, real, highest)
    partial[2 * nyp :, :] = nt(ycs, imag, highest)
    phases[: 2 * nyp, :] = ycs
    phases[2 * nyp : 2 * nyp + pairs, :] = xzc
    phases[2 * nyp + pairs :, :] = xzs
    charges[...] = q


def grid_kernel(gx, yz, nyp, latent, wave, out):
    nx = 2 * gx
    cols = out.shape[1]
    count = wave.shape[1]
    group = iota((cols, count), 0) // latent
    code = (wave[2:3, :] + z_reach) * nx + wave[0:1, :] - 1
    hot = (group == code).astype(f32).astype(bf16)
    row = iota((nyp, count), 0)
    plus = (row == wave[1:2, :]).astype(f32).astype(bf16)
    minus = ((row == -wave[1:2, :]) & (row > 0)).astype(f32).astype(bf16)
    times = nt(jnp.concatenate([plus, minus], axis=0), hot)
    ny = (iota((2 * nyp, cols), 0) % nyp).astype(f32)
    pair = iota((2 * nyp, cols), 1) // latent
    wx = ((pair % nx) + 1).astype(f32) * (two_pi / gx)
    wz = ((pair // nx) - z_reach).astype(f32) * two_pi
    wy = ny * (two_pi / yz)
    squared = wx * wx + wy * wy + wz * wz
    prefactor = 8.0 * math.pi * ewald_scale / (gx * yz)
    out[...] = times * (prefactor * jnp.exp(-0.5 * ewald_width * ewald_width * squared) / squared)


def table_kernel(work, g0, g1, g2, g3, up, table_up, table_pos):
    full = work.shape[1]
    width = full - lanes
    channels = up.shape[1]
    feat = jnp.concatenate([r[...] for r in (work, g0, g1, g2, g3)], axis=0)
    for part in range(4):
        table_up[:, part * channels : (part + 1) * channels] = mm(
            feat[:, part * channels : (part + 1) * channels], up[min(part, 1)]
        ).astype(bf16)
    lane = iota((1, lanes), 1)
    sides = [work[:, width:].astype(f32)]
    for ref, axis, shift in ((g0, 0, -1.0), (g1, 0, 1.0), (g2, 1, -1.0), (g3, 1, 1.0)):
        sides.append(ref[:, width:].astype(f32) + jnp.where(lane == axis, shift, 0.0))
    pos = jnp.concatenate(sides, axis=0).T[:8]
    high = pos.astype(bf16)
    low = (pos - high.astype(f32)).astype(bf16)
    table_pos[...] = jnp.concatenate([high.astype(f32), low.astype(f32)], axis=0).astype(bf16)


def edge_kernel(
    slots, table_up, table_pos, nbr, centre, side, prod, rin_t, mid_t, rout, products
):
    table = table_up.shape[0]
    atoms = side.shape[0]
    channels = products.shape[1] // 4
    edges = atoms * slots
    row = nbr[0]
    hot_t = (iota((table, edges), 0) == row).astype(f32).astype(bf16)
    spread = (iota((atoms, edges), 0) == iota((atoms, edges), 1) // slots).astype(f32).astype(bf16)
    both = mm(table_pos[...], hot_t)
    own = mm(centre[0], spread)
    r = both[:8] + both[8:] - own[:8]
    dist = jnp.sqrt(r[0:1] * r[0:1] + r[1:2] * r[1:2] + r[2:3] * r[2:3])
    u = dist * (1.0 / cutoff_radius)
    u2 = u * u
    u6 = u2 * u2 * u2
    env = 1.0 + u6 * (-28.0 + u * (48.0 - 21.0 * u))
    live = (iota((1, edges), 1) % slots).astype(f32) < own[4:5]
    env = jnp.where(live, env, 0.0)
    nrad = 8
    centres = iota((2 * nrad, edges), 0).astype(f32) * (cutoff_radius / (nrad - 1))
    off = dist - centres
    basis = jnp.exp(-basis_sharpness * off * off).astype(bf16)
    h = silu(mm(rin_t[...], basis)).astype(bf16)
    h = silu(mm(mid_t[0], h)).astype(bf16)
    h = silu(mm(mid_t[1], h)) * env
    cols = jnp.concatenate(
        [h, r[:3], row.astype(f32), jnp.zeros((lanes - h.shape[0] - 4, edges), f32)], axis=0
    ).T
    base = h.shape[0]
    hot = (iota((edges, table), 1).astype(f32) == cols[:, base + 3 : base + 4]).astype(f32)
    up = mm(hot.astype(bf16), table_up[...])
    radial = mm(cols[:, :base].astype(bf16), rout[...])

    def part(source, k):
        return source[:, k * channels : (k + 1) * channels]

    rm = [cols[:, base + m : base + m + 1] for m in range(3)]
    u1 = [part(up, 1 + m) for m in range(3)]
    along = rm[0] * u1[0] + rm[1] * u1[1] + rm[2] * u1[2]

    def total(v):
        return jnp.sum(v.reshape(atoms, slots, channels), axis=1) * (1.0 / math.sqrt(slots))

    a0 = total(part(radial, 0) * part(up, 0) + part(radial, 1) * along)
    ru = part(radial, 2) * part(up, 0)
    rd = part(radial, 3)
    a1 = [total(ru * rm[m] + rd * u1[m]) for m in range(3)]
    kind = side[:, 3:4].astype(f32)
    p = jnp.zeros((atoms, prod.shape[1]), f32)
    for s in range(prod.shape[0]):
        p = p + jnp.where(kind == float(s), prod[s : s + 1, :], 0.0)
    square = a1[0] * a1[0] + a1[1] * a1[1] + a1[2] * a1[2]
    b0 = part(p, 0) * a0 + part(p, 1) * a0 * a0 + part(p, 2) * square
    products[:, :channels] = b0.astype(bf16)
    for m in range(3):
        products[:, (1 + m) * channels : (2 + m) * channels] = (
            part(p, 3) * a1[m] + part(p, 4) * a0 * a1[m]
        ).astype(bf16)


def final_kernel(
    gx, yz, nyp, sums, grid, phases, charges, products, work, ow, sw, fieldw, read_t, rvec, fw,
    codes, out,
):
    channels = ow.shape[1]
    atoms = work.shape[0]
    total = sums[0]
    for d in range(1, sums.shape[0]):
        total = total + sums[d]
    cre, sre, cim, sim = [total[k * nyp : (k + 1) * nyp] for k in range(4)]
    gp, gm = grid[:nyp], grid[nyp:]
    pre, pim = gp * (cre - sim), gp * (cim + sre)
    mre, mim = gm * (cre + sim), gm * (cim - sre)
    sum_re, sum_im, dif_re, dif_im = pre + mre, pim + mim, pre - mre, pim - mim
    wy = iota(sum_re.shape, 0).astype(f32) * (two_pi / yz)
    ycs = phases[: 2 * nyp, :]
    q = charges[...]
    latent = q.shape[0]
    pairs = sum_re.shape[1] // latent

    def contract(first, second):
        left = jnp.concatenate([first, second], axis=0)
        return tn(left, ycs, highest).reshape(pairs, latent, atoms)

    v_re = contract(sum_re, dif_im)
    v_im = contract(sum_im, -dif_re)
    y_re = contract(wy * dif_re, wy * sum_im)
    y_im = contract(wy * dif_im, -wy * sum_re)
    xzc = phases[2 * nyp : 2 * nyp + pairs, :][:, None, :]
    xzs = phases[2 * nyp + pairs :, :][:, None, :]
    d_re = xzc * v_re + xzs * v_im
    d_im = xzc * v_im - xzs * v_re
    d_y = xzc * y_im - xzs * y_re
    nx = 2 * gx
    pair = iota((pairs, latent, atoms), 0)
    wx = ((pair % nx) + 1).astype(f32) * (two_pi / gx)
    wz = ((pair // nx) - z_reach).astype(f32) * two_pi
    potential = jnp.sum(d_re, axis=0)
    efield = [-jnp.sum(wx * d_im, axis=0), -jnp.sum(d_y, axis=0), -jnp.sum(wz * d_im, axis=0)]
    scal = (
        mm(products[:, :channels], ow[0])
        + mm(work[:, :channels], sw[0])
        + tn(potential, fieldw[...], highest)
    )
    readout = silu(nt(read_t[...], scal.astype(bf16)))
    energy = jnp.sum(readout * rvec[...], axis=0, keepdims=True) + 0.5 * jnp.sum(
        q * potential, axis=0, keepdims=True
    )
    rows = []
    for m in range(3):
        cut = slice((1 + m) * channels, (2 + m) * channels)
        vec = mm(products[:, cut], ow[1]) + mm(work[:, cut], sw[1])
        rows.append(
            nt(fw[...], vec, highest)[0:1] + jnp.sum(q * efield[m], axis=0, keepdims=True)
        )
    rows.append(energy)
    result = jnp.concatenate(rows + [jnp.zeros((4, atoms), f32)], axis=0)
    peers, _, block = out.shape
    for d in range(peers):
        mark = codes[d : d + 1, :block]
        acc = jnp.zeros((8, block), f32)
        for s in range(atoms // block):
            acc = acc + jnp.where(mark == s + 1.0, result[:, s * block : (s + 1) * block], 0.0)
        out[d] = acc


def home_kernel(dest, came, forces, energies):
    block = came.shape[2]
    for b in range(forces.shape[1] // block):
        got = came[dest[b]]
        forces[:, b * block : (b + 1) * block] = got[:3]
        energies[:, b * block : (b + 1) * block] = got[3:4]


def call(body, specs, out_shape, *args, **kwargs):
    many = isinstance(out_shape, (list, tuple))
    return pl.pallas_call(
        body,
        out_shape=out_shape,
        in_specs=specs,
        out_specs=[VMEM] * len(out_shape) if many else VMEM,
        **kwargs,
    )(*args)


def shape(dims, dtype):
    return jax.ShapeDtypeStruct(tuple(dims), dtype)


def on_device(
    positions,
    species,
    features,
    move_dest,
    move_slot,
    halo_list,
    neighbours,
    neighbour_count,
    wave_index,
    radial_in,
    radial_mid,
    radial_out,
    up_weight,
    prod_weight,
    out_weight,
    skip_weight,
    charge_weight,
    field_weight,
    read_weight,
    read_vector,
    force_weight,
):
    gx, yz = lax.axis_size("gx"), lax.axis_size("yz")
    atoms, width = features.shape
    blocks = move_dest.shape[0]
    block = atoms // blocks
    slots = neighbours.shape[1]
    full = width + lanes
    latent = charge_weight.shape[1]
    nyp = -(-(2 * yz + 1) // 8) * 8
    nx = 2 * gx
    pairs = nx * (2 * z_reach + 1)
    cols = pairs * latent
    halo = halo_list.shape[0]

    outgoing = call(
        send_kernel,
        [SMEM, SMEM, VMEM, VMEM, VMEM],
        shape((yz, block, full), bf16),
        move_dest,
        move_slot,
        features,
        positions,
        species.reshape(1, atoms),
    )
    recv = lax.all_to_all(outgoing, "yz", split_axis=0, concat_axis=0, tiled=True)
    work, send, codes = call(
        arrive_kernel,
        [VMEM, VMEM],
        [shape((atoms, full), bf16), shape((halo, full), bf16), shape((yz, lanes), f32)],
        recv,
        halo_list.reshape(halo, 1),
    )

    def ring(axis, step):
        count = lax.axis_size(axis)
        return lax.ppermute(send, axis, [(i, (i + step) % count) for i in range(count)])

    ghosts = [ring("gx", 1), ring("gx", -1), ring("yz", 1), ring("yz", -1)]
    grid = call(
        functools.partial(grid_kernel, gx, yz, nyp, latent),
        [VMEM],
        shape((2 * nyp, cols), f32),
        wave_index,
    )
    place = jnp.stack([lax.axis_index("gx"), lax.axis_index("yz")]).astype(f32)
    partial, phases, charges = call(
        functools.partial(wave_kernel, gx, yz, nyp),
        [SMEM, VMEM, VMEM],
        [
            shape((4 * nyp, cols), f32),
            shape((2 * nyp + 2 * pairs, atoms), f32),
            shape((latent, atoms), f32),
        ],
        place,
        work,
        charge_weight.T,
    )
    row_sums = jnp.sum(lax.all_gather(partial, "gx"), axis=0)
    sums = lax.all_gather(row_sums, "yz")
    table = atoms + 4 * halo
    table_up, table_pos = call(
        table_kernel,
        [VMEM] * 6,
        [shape((table, width), bf16), shape((16, table), bf16)],
        work,
        *ghosts,
        up_weight,
    )
    step = math.gcd(atoms, 32)
    steps = atoms // step
    edges = step * slots
    side = work[:, width:]
    own = jnp.concatenate([side[:, :4].T, neighbour_count.astype(bf16)[None]], axis=0)
    own = jnp.pad(own, ((0, 11), (0, 0))).reshape(16, steps, step).transpose(1, 0, 2)
    hidden = radial_mid.shape[1]
    nrad = radial_in.shape[0]
    rin_t = jnp.pad(radial_in.T, ((0, 0), (0, 16 - nrad)))

    def whole(a):
        return pl.BlockSpec(a.shape, lambda i: (0,) * a.ndim)

    mid_t = radial_mid.transpose(0, 2, 1)
    products = pl.pallas_call(
        functools.partial(edge_kernel, slots),
        out_shape=shape((atoms, width), bf16),
        grid=(steps,),
        in_specs=[
            whole(table_up),
            whole(table_pos),
            pl.BlockSpec((1, 1, edges), lambda i: (i, 0, 0)),
            pl.BlockSpec((1, 16, step), lambda i: (i, 0, 0)),
            pl.BlockSpec((step, lanes), lambda i: (i, 0)),
            whole(prod_weight),
            whole(rin_t),
            whole(mid_t),
            whole(radial_out),
        ],
        out_specs=pl.BlockSpec((step, width), lambda i: (i, 0)),
        compiler_params=pltpu.CompilerParams(vmem_limit_bytes=56 * 1024 * 1024),
    )(
        table_up,
        table_pos,
        neighbours.reshape(steps, 1, edges),
        own,
        side,
        prod_weight,
        rin_t,
        mid_t,
        radial_out,
    )
    back = call(
        functools.partial(final_kernel, gx, yz, nyp),
        [VMEM] * 13,
        shape((yz, 8, block), f32),
        sums,
        grid,
        phases,
        charges,
        products,
        work,
        out_weight,
        skip_weight,
        field_weight,
        read_weight.T,
        read_vector.reshape(-1, 1),
        jnp.broadcast_to(force_weight[None], (8, force_weight.shape[0])),
        codes,
    )
    came = lax.all_to_all(back, "yz", split_axis=0, concat_axis=0, tiled=True)
    forces, energies = call(
        home_kernel,
        [SMEM, VMEM],
        [shape((3, atoms), f32), shape((1, atoms), f32)],
        move_dest,
        came,
    )
    return (forces, energies.reshape(atoms))


def solution(mesh):
    split = P(("gx", "yz"))
    rows = P(("gx", "yz"), None)
    in_specs = (P(None, ("gx", "yz")), split, rows, split, split, split, rows, split) + (P(),) * 13
    out_specs = (P(None, ("gx", "yz")), split)
    return jax.shard_map(
        on_device, mesh=mesh, in_specs=in_specs, out_specs=out_specs, check_vma=False
    )
```

profile of v0, /device:TPU:0, one launch (start us, length us, event | category | flops | bytes accessed | tf_op | source)
XLA Modules:
  0.0 119.9 jit_solution(17211583993821936482)
XLA Ops:
  0.6 2.7 %shard_map.212 = bf16[8,128,640]{2,1,0:T(8,128)(2,1)} custom-call(s32[2]{0:T(128)} %dest.3, s32[2]{0:T(128)} %slot.1, bf16[256,512]{1,0:T(8,128)(2,1)} %feat.1, bf16[3,256]{1,0:T(4,128)(2,1)} %pos.1, s32[1,256]{1,0:T(1,128)} %bitcast.24), custom_call_target="tpu_custom_call" | custom-call | tf_op jit(solution)/shard_map/pallas_call | solution.py:308
  3.3 0.0 copy-start.8
  3.3 0.0 copy-start.11
  3.3 0.0 copy-start.1
  3.3 0.0 copy-start.6
  3.4 0.0 copy-start.7
  3.4 0.0 copy-start.9
  3.4 5.3 %all-to-all-start = ((bf16[8,128,640]{2,1,0:T(8,128)(2,1)}), bf16[8,128,640]{2,1,0:T(8,128)(2,1)S(1)}, u32[]{:S(2)}, u32[]{:S(2)}) async-start(bf16[8,128,640]{2,1,0:T(8,128)(2,1)} %shard_map.212), calls=%async_computation | async-start | bytes 2621440 | tf_op jit(solution)/shard_map/all_to_all | solution.py:367
  8.7 0.0 copy-done.8
  8.7 0.7 copy.37.halo
  9.4 0.0 copy-done.11
  9.4 0.0 copy-done.1
  9.4 0.1 copy.38
  9.5 0.8 reshape.31.nbr
  10.3 0.0 copy-done.6
  10.3 0.7 copy.42
  11.0 0.0 copy-done.7
  11.0 0.1 copy.41
  11.1 2.3 %shard_map.215.grid = f32[48,320]{1,0:T(8,128)} custom-call(s32[3,4096]{1,0:T(4,128)} %wave.1), custom_call_target="tpu_custom_call" | custom-call | tf_op jit(solution)/shard_map/pallas_call | solution.py:308
  13.4 0.0 copy-done.9
  13.4 0.7 copy.44.rvec
  14.1 0.6 pad.9.rin_t
  14.7 0.6 add_convert_fusion.place
  15.4 11.5 %all-to-all-done.recv = bf16[8,128,640]{2,1,0:T(8,128)(2,1)S(1)} async-done(((bf16[8,128,640]{2,1,0:T(8,128)(2,1)}), bf16[8,128,640]{2,1,0:T(8,128)(2,1)S(1)}, u32[]{:S(2)}, u32[]{:S(2)}) %all-to-all-start) | async-done | bytes 1310752 | tf_op jit(solution)/shard_map/all_to_all | solution.py:367
  26.9 0.0 copy-start
  26.9 1.1 copy-done
  28.0 2.8 %shard_map.213 = (bf16[256,640]{1,0:T(8,128)(2,1)}, bf16[32,640]{1,0:T(8,128)(2,1)}, f32[8,128]{1,0:T(8,128)}) custom-call(bf16[8,128,640]{2,1,0:T(8,128)(2,1)} %copy-done, s32[32,1]{1,0:T(8,128)} %copy.37.halo), custom_call_target="tpu_custom_call" | custom-call | tf_op jit(solution)/shard_map/pallas_call | solution.py:308
  30.8 1.6 %collective-permute-start = (bf16[32,640]{1,0:T(8,128)(2,1)}, bf16[32,640]{1,0:T(8,128)(2,1)S(1)}, u32[]{:S(2)}, u32[]{:S(2)}) collective-permute-start(bf16[32,640]{1,0:T(8,128)(2,1)} %get-tuple-element.16), channel_id=1, source_target_pairs={{0,8},{8,16},{16,24},{24,0},{1,9},{9,17},{17,25},{25,1},{2,10},{10... | collective-permute-start | bytes 122888 | tf_op jit(solution)/shard_map/ppermute | solution.py:378
  32.3 2.2 %collective-permute-start.1 = (bf16[32,640]{1,0:T(8,128)(2,1)}, bf16[32,640]{1,0:T(8,128)(2,1)S(1)}, u32[]{:S(2)}, u32[]{:S(2)}) collective-permute-start(bf16[32,640]{1,0:T(8,128)(2,1)} %get-tuple-element.16), channel_id=1, source_target_pairs={{0,24},{8,0},{16,8},{24,16},{1,25},{9,1},{17,9},{25,17},{2,26},{10... | collective-permute-start | bytes 122888 | tf_op jit(solution)/shard_map/ppermute | solution.py:378
  34.6 0.0 collective-permute-start.2
  34.6 2.6 %collective-permute-start.3 = (bf16[32,640]{1,0:T(8,128)(2,1)}, bf16[32,640]{1,0:T(8,128)(2,1)S(1)}, u32[]{:S(2)}, u32[]{:S(2)}) collective-permute-start(bf16[32,640]{1,0:T(8,128)(2,1)} %get-tuple-element.16), channel_id=1, source_target_pairs={{0,7},{1,0},{2,1},{3,2},{4,3},{5,4},{6,5},{7,6},{8,15},{9,8},{10,9... | collective-permute-start | bytes 122888 | tf_op jit(solution)/shard_map/ppermute | solution.py:378
  37.2 0.8 slice_bitcast_fusion
  38.1 0.1 copy.39
  38.2 2.8 %shard_map.214 = (f32[96,320]{1,0:T(8,128)}, f32[128,256]{1,0:T(8,128)}, f32[8,256]{1,0:T(8,128)}) custom-call(f32[2]{0:T(128)} %add_convert_fusion.place, bf16[256,640]{1,0:T(8,128)(2,1)} %get-tuple-element.12.work, bf16[8,128]{1,0:T(8,128)(2,1)} %bitcast.23), custom_call_target="tpu_custom_call" | custom-call | tf_op jit(solution)/shard_map/pallas_call | solution.py:308
  40.9 16.5 %all-gather = f32[384,320]{1,0:T(8,128)S(1)} all-gather(f32[96,320]{1,0:T(8,128)} %get-tuple-element.13), channel_id=2, replica_groups=mesh['gx'=4,'yz'=8] {'gx'}, dimensions={0}, use_global_device_ids=true | all-gather | bytes 614400 | tf_op jit(solution)/shard_map/all_gather | solution.py:400
  57.4 0.0 copy-start.10
  57.4 11.3 %all-gather.1 = f32[768,320]{1,0:T(8,128)} all-gather(f32[96,320]{1,0:T(8,128)S(1)} %reduce_sum.9), channel_id=3, replica_groups=mesh['gx'=4,'yz'=8] {'yz'}, dimensions={0}, use_global_device_ids=true | all-gather | bytes 1105920 | tf_op jit(solution)/shard_map/all_gather | solution.py:401
  68.8 1.5 %slice.8.side = bf16[256,128]{1,0:T(8,128)(2,1)} slice(bf16[256,640]{1,0:T(8,128)(2,1)} %get-tuple-element.12.work), slice={[0:256], [512:640]} | slice | bytes 131072 | tf_op jit(solution)/shard_map/slice | solution.py:414
  70.2 0.1 reshape.26
  70.3 0.6 copy.46
  71.0 0.0 collective-permute-done.g0
  71.0 0.0 copy-start.2
  71.0 0.0 collective-permute-done.1.g1
  71.0 0.0 copy-start.3
  71.0 0.0 collective-permute-done.2.g2
  71.0 0.0 copy-start.4
  71.0 0.0 collective-permute-done.3.g3
  71.0 0.6 copy-done.2
  71.6 0.0 copy-done.3
  71.6 0.0 copy-done.4
  71.6 0.0 copy-start.5
  71.6 0.6 copy-done.5
  72.2 2.0 %shard_map.216 = (bf16[384,512]{1,0:T(8,128)(2,1)}, bf16[16,384]{1,0:T(8,128)(2,1)}) custom-call(bf16[256,640]{1,0:T(8,128)(2,1)} %get-tuple-element.12.work, bf16[32,640]{1,0:T(8,128)(2,1)} %copy-done.2, bf16[32,640]{1,0:T(8,128)(2,1)} %copy-done.3, bf16[32,640]{1,0:T(8,128)(2,1)} %copy-done.4, bf16[32,640]{1,0:T(8,128)(2,1)} %copy-done.5, ...), custom_call_target="tpu_custom_call" | custom-call | tf_op jit(solution)/shard_map/pallas_call | solution.py:308
  74.2 30.3 %shard_map.217.products = bf16[256,512]{1,0:T(8,128)(2,1)} custom-call(bf16[384,512]{1,0:T(8,128)(2,1)} %get-tuple-element.17.table_up, bf16[16,384]{1,0:T(8,128)(2,1)} %get-tuple-element.18.table_pos, s32[8,1,2048]{2,1,0:T(1,128)} %reshape.31.nbr, bf16[8,16,32]{2,1,0:T(8,128)(2,1)} %bitcast.20, bf16[256,128]{1,0:T(8,128)(2,1)} %slice.8.side, ...), custom_call_target="tpu_custom_call" | custom-call | tf_op jit(solution)/shard_map/pallas_call | solution.py:425
  104.5 0.0 copy-done.10
  104.5 0.6 broadcast_in_dim.10.fw
  105.1 4.6 %shard_map.218 = f32[8,8,128]{2,1,0:T(8,128)} custom-call(f32[8,96,320]{2,1,0:T(8,128)} %bitcast.17, f32[48,320]{1,0:T(8,128)} %shard_map.215.grid, f32[128,256]{1,0:T(8,128)} %get-tuple-element.14.phases, f32[8,256]{1,0:T(8,128)} %get-tuple-element.15.charges, bf16[256,512]{1,0:T(8,128)(2,1)} %shard_map.217.products, ...), custom_call_target="tpu_custom_call" | custom-call | tf_op jit(solution)/shard_map/pallas_call | solution.py:308
  109.7 8.8 %all_to_all.10.came = f32[8,8,128]{2,1,0:T(8,128)} all-to-all(f32[8,8,128]{2,1,0:T(8,128)} %shard_map.218), channel_id=1, replica_groups=mesh['gx'=4,'yz'=8] {'yz'}, dimensions={0} | all-to-all | bytes 65536 | tf_op jit(solution)/shard_map/all_to_all | solution.py:471
  118.5 1.4 %shard_map.219 = (f32[3,256]{1,0:T(4,128)}, f32[1,256]{1,0:T(1,128)}) custom-call(s32[2]{0:T(128)} %dest.3, f32[8,8,128]{2,1,0:T(8,128)} %all_to_all.10.came), custom_call_target="tpu_custom_call" | custom-call | tf_op jit(solution)/shard_map/pallas_call | solution.py:308
  (4 shorter events, 0.1 us)
Async XLA Ops:
  3.3 5.4 %copy-start.8 = (s32[32]{0:T(128)S(1)}, s32[32]{0:T(128)}, u32[]{:S(2)}) copy-start(s32[32]{0:T(128)} %param.26) | copy-start | bytes 388
  3.3 6.1 %copy-start.11 = (s32[256]{0:T(256)S(1)}, s32[256]{0:T(256)}, u32[]{:S(2)}) copy-start(s32[256]{0:T(256)} %param.28) | copy-start | bytes 3076
  3.3 6.1 %copy-start.1 = (s32[256,64]{0,1:T(8,128)S(1)}, s32[256,64]{0,1:T(8,128)}, u32[]{:S(2)}) copy-start(s32[256,64]{0,1:T(8,128)} %param.27) | copy-start | bytes 196612
  3.3 6.9 %copy-start.6 = (bf16[2,64,64]{2,1,0:T(8,128)(2,1)S(1)}, bf16[2,64,64]{2,1,0:T(8,128)(2,1)}, u32[]{:S(2)}) copy-start(bf16[2,64,64]{2,1,0:T(8,128)(2,1)} %param.31) | copy-start | bytes 49156
  3.4 7.6 %copy-start.7 = (bf16[8,64]{1,0:T(8,128)(2,1)S(1)}, bf16[8,64]{1,0:T(8,128)(2,1)}, u32[]{:S(2)}) copy-start(bf16[8,64]{1,0:T(8,128)(2,1)} %param.30) | copy-start | bytes 3076
  3.4 10.1 %copy-start.9 = (f32[16]{0:T(128)S(1)}, f32[16]{0:T(128)}, u32[]{:S(2)}) copy-start(f32[16]{0:T(128)} %param.40) | copy-start | bytes 196
  3.4 23.5 %all-to-all-start = ((bf16[8,128,640]{2,1,0:T(8,128)(2,1)}), bf16[8,128,640]{2,1,0:T(8,128)(2,1)S(1)}, u32[]{:S(2)}, u32[]{:S(2)}) async-start(bf16[8,128,640]{2,1,0:T(8,128)(2,1)} %shard_map.212), calls=%async_computation | async-start | bytes 2621440 | tf_op jit(solution)/shard_map/all_to_all | solution.py:367
  26.9 1.1 copy-start
  30.8 40.2 %collective-permute-start = (bf16[32,640]{1,0:T(8,128)(2,1)}, bf16[32,640]{1,0:T(8,128)(2,1)S(1)}, u32[]{:S(2)}, u32[]{:S(2)}) collective-permute-start(bf16[32,640]{1,0:T(8,128)(2,1)} %get-tuple-element.16), channel_id=1, source_target_pairs={{0,8},{8,16},{16,24},{24,0},{1,9},{9,17},{17,25},{25,1},{2,10},{10... | collective-permute-start | bytes 122888 | tf_op jit(solution)/shard_map/ppermute | solution.py:378
  32.3 38.6 %collective-permute-start.1 = (bf16[32,640]{1,0:T(8,128)(2,1)}, bf16[32,640]{1,0:T(8,128)(2,1)S(1)}, u32[]{:S(2)}, u32[]{:S(2)}) collective-permute-start(bf16[32,640]{1,0:T(8,128)(2,1)} %get-tuple-element.16), channel_id=1, source_target_pairs={{0,24},{8,0},{16,8},{24,16},{1,25},{9,1},{17,9},{25,17},{2,26},{10... | collective-permute-start | bytes 122888 | tf_op jit(solution)/shard_map/ppermute | solution.py:378
  34.6 36.4 %collective-permute-start.2 = (bf16[32,640]{1,0:T(8,128)(2,1)}, bf16[32,640]{1,0:T(8,128)(2,1)S(1)}, u32[]{:S(2)}, u32[]{:S(2)}) collective-permute-start(bf16[32,640]{1,0:T(8,128)(2,1)} %get-tuple-element.16), channel_id=1, source_target_pairs={{0,1},{1,2},{2,3},{3,4},{4,5},{5,6},{6,7},{7,0},{8,9},{9,10},{10,1... | collective-permute-start | bytes 122888 | tf_op jit(solution)/shard_map/ppermute | solution.py:378
  34.6 36.4 %collective-permute-start.3 = (bf16[32,640]{1,0:T(8,128)(2,1)}, bf16[32,640]{1,0:T(8,128)(2,1)S(1)}, u32[]{:S(2)}, u32[]{:S(2)}) collective-permute-start(bf16[32,640]{1,0:T(8,128)(2,1)} %get-tuple-element.16), channel_id=1, source_target_pairs={{0,7},{1,0},{2,1},{3,2},{4,3},{5,4},{6,5},{7,6},{8,15},{9,8},{10,9... | collective-permute-start | bytes 122888 | tf_op jit(solution)/shard_map/ppermute | solution.py:378
  57.4 47.1 %copy-start.10 = (f32[128]{0:T(128)S(1)}, f32[128]{0:T(128)}, u32[]{:S(2)}) copy-start(f32[128]{0:T(128)} %param.41) | copy-start | bytes 1540
  71.0 0.6 copy-start.2
  71.0 0.6 copy-start.3
  71.0 0.6 copy-start.4
  71.6 0.6 copy-start.5
where the time goes:
time: 121 us; the launch traced here: 120 us
  Pallas kernels  48.9 us (40%)
  blocking collectives  36.6 us (30%)
  starting transfers between devices  11.8 us (10%)
  waiting for transfers between devices  11.5 us (10%)
  local copies, waits for them, and re-layouts  9.67 us (8%)
    pallas_call x1, Pallas kernels, on_device(): pl.pallas_call(functools.partial(edge_kernel, slots), out_shape=shape((at...  30.3 us
    pallas_call x7, Pallas kernels, call(): pl.pallas_call(body, out_shape=out_shape, in_specs=specs, out_specs=[VMEM...  18.6 us
    all_gather x1, blocking collectives, on_device(): row_sums = jnp.sum(lax.all_gather(partial, 'gx'), axis=0)  16.5 us
    all_to_all x1, waiting for transfers between devices, on_device(): lax.all_to_all(outgoing, 'yz', split_axis=0, concat_axis=0, tiled=True)  11.5 us
    all_gather x1, blocking collectives, on_device(): sums = lax.all_gather(row_sums, 'yz')  11.3 us
    all_to_all x1, blocking collectives, on_device(): came = lax.all_to_all(back, 'yz', split_axis=0, concat_axis=0, tiled=True)  8.77 us
    ppermute x4, starting transfers between devices, ring(): lax.ppermute(send, axis, [(i, (i + step) % count) for i in range(count)])  6.47 us
    all_to_all x1, starting transfers between devices, on_device(): lax.all_to_all(outgoing, 'yz', split_axis=0, concat_axis=0, tiled=True)  5.34 us
  transfers between devices with their start and end apart: 5, of which 1 were waited for; matrix products, arithmetic and copies ran while one was open for 6% of the time, Pallas kernels for 4%

commit v1 on v0

v1 whole, which is shorter than its diff:
```python
import functools
import math

import jax
import jax.numpy as jnp
from jax import lax
from jax.experimental import pallas as pl
from jax.experimental.pallas import tpu as pltpu
from jax.sharding import PartitionSpec as P

highest = lax.Precision.HIGHEST
two_pi = 2.0 * math.pi
cutoff_radius = 3.5
basis_sharpness = 4.0
ewald_width = 0.1
ewald_scale = 0.01
z_reach = 2
lanes = 128
group = 8
f32 = jnp.float32
bf16 = jnp.bfloat16
i32 = jnp.int32

VMEM = pl.BlockSpec(memory_space=pltpu.VMEM)
SMEM = pl.BlockSpec(memory_space=pltpu.SMEM)
MESH = pl.DeviceIdType.MESH
NT = (((1,), (1,)), ((), ()))
TN = (((0,), (0,)), ((), ()))


def nt(a, b, precision=None):
    return lax.dot_general(a, b, NT, precision=precision, preferred_element_type=f32)


def tn(a, b, precision=None):
    return lax.dot_general(a, b, TN, precision=precision, preferred_element_type=f32)


def mm(a, b, precision=None):
    return jnp.dot(a, b, precision=precision, preferred_element_type=f32)


def iota(shape, dim):
    return lax.broadcasted_iota(jnp.int32, shape, dim)


def silu(v):
    half = 0.5 * v
    return half + half * jnp.tanh(half)


def turn_cos_sin(turns):
    frac = turns - jnp.floor(turns + 0.5)
    angle = two_pi * frac
    return jnp.cos(angle), jnp.sin(angle)


def flip(a):
    return a.astype(f32).T.astype(a.dtype)


def step_kernel(
    sizes,
    dest, slot, pos, species, feat, halo, nbr, count, wave, rin, mid, rout, up, prod, ow, sw,
    charge, fieldw, readw, rvec, fw,
    out,
    meta_in, meta_out, meta_got, feat_out, feat_got, work,
    halo_pos, ghost_pos, halo_feat, ghost_feat,
    xz, ymat, dmat, part_out, part_got, row_sum, row_got, coef, coefs,
    nbr_t, rel, hidden, table_t, acc, back, came,
    meta_s, meta_r, feat_s, feat_r, hp_s, hp_r, hf_s, hf_r, rs_s, rs_r, gs_s, gs_r, ag_s, ag_r,
    ret_s, ret_r,
):
    gx, yz, nyp = sizes
    row, me = lax.axis_index("gx"), lax.axis_index("yz")
    atoms, width = feat.shape
    channels = width // 4
    blocks = dest.shape[0]
    block = atoms // blocks
    slots = nbr.shape[1]
    groups = slots // group
    latent = charge.shape[1]
    nx = 2 * gx
    pairs = nx * (2 * z_reach + 1)
    share = pairs * latent // yz
    halos = halo.shape[1]
    width_y = ymat.shape[0]

    def peer(k):
        return lax.rem(me + k, yz)

    def row_peer(k):
        return lax.rem(row + k, gx)

    def to_yz(src, dst, s, r, k):
        return pltpu.make_async_remote_copy(
            src_ref=src, dst_ref=dst, send_sem=s, recv_sem=r,
            device_id={"yz": peer(k)}, device_id_type=MESH,
        )

    def to_gx(src, dst, s, r, k):
        return pltpu.make_async_remote_copy(
            src_ref=src, dst_ref=dst, send_sem=s, recv_sem=r,
            device_id={"gx": row_peer(k)}, device_id_type=MESH,
        )

    barrier = pltpu.get_barrier_semaphore()
    for k in range(1, yz):
        pl.semaphore_signal(barrier, inc=1, device_id={"yz": peer(k)}, device_id_type=MESH)
    for k in range(1, gx):
        pl.semaphore_signal(barrier, inc=1, device_id={"gx": row_peer(k)}, device_id_type=MESH)

    meta_in[...] = jnp.concatenate(
        [pos[...].astype(f32), species[...].astype(f32), jnp.zeros((4, atoms), f32)], axis=0
    )
    line = iota((8, block), 0)
    for d in range(yz):
        picked = jnp.zeros((block, width), bf16)
        record = jnp.zeros((8, block), f32)
        for b in range(blocks):
            cut = slice(b * block, (b + 1) * block)
            hit = jnp.where(jnp.full((1, 1), dest[b], i32) == d, 1.0, 0.0)
            mark = (slot[b] + 1).astype(f32)
            picked = picked + hit.astype(bf16) * feat[cut, :]
            record = record + hit * jnp.where(line == 4, mark, meta_in[:, cut])
        feat_out[d] = picked
        meta_out[d] = record
    pl.semaphore_wait(barrier, yz - 1 + gx - 1)

    meta_copies, feat_copies = [], []
    for k in range(1, yz):
        c = to_yz(meta_out.at[peer(k)], meta_got.at[k], meta_s.at[k], meta_r.at[k], k)
        c.start()
        meta_copies.append(c)
    for k in range(1, yz):
        c = to_yz(feat_out.at[peer(k)], feat_got.at[k], feat_s.at[k], feat_r.at[k], k)
        c.start()
        feat_copies.append(c)
    sent = meta_copies + feat_copies

    for g in range(groups):
        nbr_t[g] = nbr[...].astype(f32).T[g * group : (g + 1) * group, :].astype(i32)
    rin_t = jnp.concatenate([rin[...].astype(f32), jnp.zeros_like(rin, f32)], axis=0).T.astype(bf16)
    mid_t = [flip(mid[i]) for i in range(2)]
    rout_t = flip(rout[...])

    codes = (wave[2:3, :] + z_reach) * nx + wave[0:1, :] - 1
    waves = wave.shape[1]
    hot = ((me * share + iota((share, waves), 0)) // latent == codes).astype(f32).astype(bf16)
    level = iota((nyp, waves), 0)
    plus = (level == wave[1:2, :]).astype(f32).astype(bf16)
    minus = ((level == -wave[1:2, :]) & (level > 0)).astype(f32).astype(bf16)
    pair = (me * share + iota((share, nyp), 0)) // latent
    wx = ((pair % nx) + 1).astype(f32) * (two_pi / gx)
    wz = ((pair // nx) - z_reach).astype(f32) * two_pi
    wy = iota((share, nyp), 1).astype(f32) * (two_pi / yz)
    squared = wx * wx + wy * wy + wz * wz
    prefactor = 8.0 * math.pi * ewald_scale / (gx * yz)
    weight = prefactor * jnp.exp(-0.5 * ewald_width * ewald_width * squared) / squared
    gp, gm = weight * nt(hot, plus), weight * nt(hot, minus)

    for c in meta_copies:
        c.wait_recv()
    meta_got[0] = meta_out[me]
    metas = []
    for s in range(blocks):
        total = jnp.zeros((8, block), f32)
        for k in range(yz):
            got = meta_got[k]
            total = total + jnp.where(got[4:5, :] == s + 1.0, got, 0.0)
        metas.append(total)
    meta = jnp.concatenate(metas, axis=1)

    list4 = jnp.concatenate([halo[...]] * 4, axis=1)
    pick_t = (iota((atoms, 4 * halos), 0) == list4).astype(f32)
    halo_pos[...] = mm(meta.astype(bf16), pick_t.astype(bf16))
    pick = pick_t.T[:halos].astype(bf16)
    ways = ((to_gx, 1, gx), (to_gx, gx - 1, gx), (to_yz, 1, yz), (to_yz, yz - 1, yz))
    ghost_copies = []
    for i, (send, k, n) in enumerate(ways):
        c = send(halo_pos, ghost_pos.at[i], hp_s.at[i], hp_r.at[i], k)
        c.start()
        ghost_copies.append(c)
    sent += ghost_copies

    x_turns = (meta[0:1] + row.astype(f32)) * (1.0 / gx)
    y_turns = (meta[1:2] + me.astype(f32)) * (1.0 / yz)
    xc, xs = turn_cos_sin((iota((nx, atoms), 0) + 1).astype(f32) * x_turns)
    zc, zs = turn_cos_sin((iota((8, atoms), 0) - z_reach).astype(f32) * meta[2:3])
    yc, ys = turn_cos_sin(iota((nyp, atoms), 0).astype(f32) * y_turns)
    for m in range(2 * z_reach + 1):
        c1, s1 = zc[m : m + 1], zs[m : m + 1]
        xz[0, m * nx : (m + 1) * nx, :] = xc * c1 - xs * s1
        xz[1, m * nx : (m + 1) * nx, :] = xc * s1 + xs * c1
    ymat[...] = jnp.zeros_like(ymat)
    dmat[...] = jnp.zeros_like(dmat)
    wide = iota((nyp, atoms), 0).astype(f32) * (two_pi / yz)
    for half in range(2):
        cut = slice(half * atoms, (half + 1) * atoms)
        sign = -1.0 if half == 0 else 1.0
        base = 2 * half * nyp
        ymat[base : base + nyp, cut] = yc
        ymat[base + nyp : base + 2 * nyp, cut] = ys
        dmat[base : base + nyp, cut] = sign * wide * ys
        dmat[base + nyp : base + 2 * nyp, cut] = -sign * wide * yc

    for c in ghost_copies:
        c.wait_recv()
    part = iota((8, 4 * halos), 1) // halos
    lead = iota((8, 4 * halos), 0)
    ghosts = jnp.zeros((8, 4 * halos), f32)
    for i, (axis, shift) in enumerate(((0, -1.0), (0, 1.0), (1, -1.0), (1, 1.0))):
        ghosts = jnp.where(part == i, ghost_pos[i] + jnp.where(lead == axis, shift, 0.0), ghosts)
    table_pos = jnp.concatenate([meta, ghosts], axis=1)
    table = table_pos.shape[1]
    counts = count[...]
    nrad = rin.shape[0]
    centres = iota((2 * nrad, atoms), 0).astype(f32) * (cutoff_radius / (nrad - 1))

    def radial_step(g, carry):
        index = nbr_t[g]
        local = index % lanes
        place = index // lanes
        rs = []
        for m in range(3):
            cols = []
            for h in range(atoms // lanes):
                cut = slice(h * lanes, (h + 1) * lanes)
                found = jnp.zeros((group, lanes), f32)
                for t in range(table // lanes):
                    piece = jnp.broadcast_to(
                        table_pos[m : m + 1, t * lanes : (t + 1) * lanes], (group, lanes)
                    )
                    got = jnp.take_along_axis(piece, local[:, cut], axis=1, mode="promise_in_bounds")
                    found = jnp.where(place[:, cut] == t, got, found)
                cols.append(found)
            r = jnp.concatenate(cols, axis=1) - meta[m : m + 1]
            rel[g, m] = r
            rs.append(r)
        dist = jnp.sqrt(rs[0] * rs[0] + rs[1] * rs[1] + rs[2] * rs[2])
        u = dist * (1.0 / cutoff_radius)
        u2 = u * u
        u6 = u2 * u2 * u2
        env = 1.0 + u6 * (-28.0 + u * (48.0 - 21.0 * u))
        live = (iota((group, atoms), 0) + g * group) < counts
        env = jnp.where(live, env, 0.0)
        basis = []
        for s in range(group):
            off = dist[s : s + 1] - centres
            basis.append(jnp.exp(-basis_sharpness * off * off))
        h = silu(mm(rin_t, jnp.concatenate(basis, axis=1).astype(bf16))).astype(bf16)
        h = silu(mm(mid_t[0], h)).astype(bf16)
        h = silu(mm(mid_t[1], h))
        for s in range(group):
            hidden[g, s] = (h[:, s * atoms : (s + 1) * atoms] * env[s : s + 1]).astype(bf16)
        return carry

    lax.fori_loop(0, groups, radial_step, 0)

    for c in feat_copies:
        c.wait_recv()
    feat_got[0] = feat_out[me]
    for s in range(blocks):
        total = jnp.zeros((block, width), bf16)
        for k in range(yz):
            hit = (meta_got[k, 4:5, 0:1] == s + 1.0).astype(f32).astype(bf16)
            total = total + hit * feat_got[k]
        work[s * block : (s + 1) * block, :] = total
    halo_feat[...] = mm(pick, work[...]).astype(bf16)
    halo_copies = []
    for i, (send, k, n) in enumerate(ways):
        c = send(halo_feat, ghost_feat.at[i], hf_s.at[i], hf_r.at[i], k)
        c.start()
        halo_copies.append(c)
    sent += halo_copies

    scalars = work[:, :channels]
    q = nt(flip(charge[...]), scalars)
    weighted = [
        (xz[i][:, None, :] * q[None]).reshape(pairs * latent, atoms) for i in range(2)
    ]
    part_out[...] = nt(jnp.concatenate(weighted, axis=1), ymat[...], highest).reshape(
        yz, share, width_y
    )
    part_copies = []
    for k in range(1, yz):
        c = to_yz(part_out.at[peer(k)], part_got.at[k], rs_s.at[k], rs_r.at[k], k)
        c.start()
        part_copies.append(c)
    sent += part_copies

    def raise_rows(rows, start, size):
        for p in range(4):
            cut = slice(p * channels, (p + 1) * channels)
            got = mm(rows[:, cut], up[min(p, 1)])
            table_t[cut, start : start + size] = got.T.astype(bf16)

    raise_rows(work[...], 0, atoms)
    for c in halo_copies:
        c.wait_recv()
    raise_rows(
        jnp.concatenate([ghost_feat[i] for i in range(4)], axis=0), atoms, 4 * halos
    )

    acc[...] = jnp.zeros_like(acc)

    def message_step(g, carry):
        index = nbr_t[g]
        r = [rel[g, m] for m in range(3)]
        for s in range(group):
            hot_t = (iota((table, atoms), 0) == index[s : s + 1]).astype(f32).astype(bf16)
            u = mm(table_t[...], hot_t)
            radial = mm(rout_t, hidden[g, s])
            us = [u[p * channels : (p + 1) * channels] for p in range(4)]
            rads = [radial[p * channels : (p + 1) * channels] for p in range(4)]
            rm = [r[m][s : s + 1] for m in range(3)]
            along = rm[0] * us[1] + rm[1] * us[2] + rm[2] * us[3]
            acc[0] += rads[0] * us[0] + rads[1] * along
            ru = rads[2] * us[0]
            for m in range(3):
                acc[1 + m] += ru * rm[m] + rads[3] * us[1 + m]
        return carry

    first, second = groups // 3, 2 * groups // 3
    lax.fori_loop(0, first, message_step, 0)

    for c in part_copies:
        c.wait_recv()
    total = part_out[me]
    for k in range(1, yz):
        total = total + part_got[k]
    row_sum[...] = total
    row_copies = []
    for k in range(1, gx):
        c = to_gx(row_sum, row_got.at[k], gs_s.at[k], gs_r.at[k], k)
        c.start()
        row_copies.append(c)
    sent += row_copies

    lax.fori_loop(first, second, message_step, 0)

    for c in row_copies:
        c.wait_recv()
    total = row_sum[...]
    for k in range(1, gx):
        total = total + row_got[k]
    quarters = [total[:, i * nyp : (i + 1) * nyp] for i in range(4)]
    rest = jnp.zeros((share, width_y - 4 * nyp), f32)
    both, gap = gp + gm, gp - gm
    coef[...] = jnp.concatenate(
        [
            both * quarters[0] - gap * quarters[3],
            both * quarters[1] + gap * quarters[2],
            both * quarters[2] + gap * quarters[1],
            both * quarters[3] - gap * quarters[0],
            rest,
        ],
        axis=1,
    )
    coef_copies = []
    for k in range(1, yz):
        c = to_yz(coef, coefs.at[me], ag_s.at[k], ag_r.at[k], k)
        c.start()
        coef_copies.append(c)
    coefs[me] = coef[...]
    sent += coef_copies

    lax.fori_loop(second, groups, message_step, 0)

    scale = 1.0 / math.sqrt(slots)
    kinds = prod.shape[0]
    kind = meta[3:4]
    which = (iota((8, atoms), 0).astype(f32) == kind).astype(f32).astype(bf16)
    weights = prod[...]
    high = weights.astype(bf16).astype(f32)
    middle = (weights - high).astype(bf16).astype(f32)
    low = weights - high - middle
    gap_rows = jnp.zeros((8 - kinds, weights.shape[1]), f32)
    stack = jnp.concatenate([high, gap_rows, middle, gap_rows, low, gap_rows], axis=0)
    p_t = tn(stack.astype(bf16), jnp.concatenate([which] * 3, axis=0))
    p = [p_t[i * channels : (i + 1) * channels] for i in range(5)]
    a0 = acc[0] * scale
    a1 = [acc[1 + m] * scale for m in range(3)]
    square = a1[0] * a1[0] + a1[1] * a1[1] + a1[2] * a1[2]
    b0 = (p[0] * a0 + p[1] * a0 * a0 + p[2] * square).astype(bf16)
    b1 = [(p[3] * a1[m] + p[4] * a0 * a1[m]).astype(bf16) for m in range(3)]

    for c in coef_copies:
        c.wait_recv()
    full = coefs[...].reshape(yz * share, width_y)
    v = mm(full, ymat[...], highest)
    vy = mm(full, dmat[...], highest)
    v_re, v_im = v[:, :atoms], v[:, atoms:]
    y_im, y_re = vy[:, :atoms], vy[:, atoms:]
    zero = jnp.zeros((latent, atoms), f32)
    potential, field = zero, [zero, zero, zero]
    for j in range(pairs):
        cut = slice(j * latent, (j + 1) * latent)
        cos_row, sin_row = xz[0, j : j + 1], xz[1, j : j + 1]
        d_im = cos_row * v_im[cut] - sin_row * v_re[cut]
        potential = potential + (cos_row * v_re[cut] + sin_row * v_im[cut])
        field[0] = field[0] - ((j % nx) + 1) * (two_pi / gx) * d_im
        field[1] = field[1] - (cos_row * y_im[cut] - sin_row * y_re[cut])
        field[2] = field[2] - ((j // nx) - z_reach) * two_pi * d_im

    scal = (
        tn(ow[0], b0)
        + mm(scalars, sw[0]).T
        + tn(fieldw[...], potential, highest)
    )
    readout = silu(tn(readw[...], scal.astype(bf16)))
    tall = jnp.broadcast_to(rvec[...], (8, rvec.shape[1]))
    energy = mm(tall, readout, highest)[0:1] + 0.5 * jnp.sum(q * potential, axis=0, keepdims=True)
    force8 = jnp.broadcast_to(fw[...], (8, channels))
    to_b = nt(force8, ow[1].astype(f32), highest)
    to_f = nt(force8, sw[1].astype(f32), highest)
    rows = []
    for m in range(3):
        cut = slice((1 + m) * channels, (2 + m) * channels)
        rows.append(
            mm(to_b, b1[m].astype(f32), highest)[0:1]
            + nt(to_f, work[:, cut].astype(f32), highest)[0:1]
            + jnp.sum(q * field[m], axis=0, keepdims=True)
        )
    result = jnp.concatenate(rows + [energy, jnp.zeros((4, atoms), f32)], axis=0)
    for k in range(yz):
        mark = meta_got[k, 4:5, :]
        total = jnp.zeros((8, block), f32)
        for s in range(blocks):
            total = total + jnp.where(mark == s + 1.0, result[:, s * block : (s + 1) * block], 0.0)
        back[k] = total
    back_copies = []
    for k in range(1, yz):
        c = to_yz(back.at[k], came.at[k], ret_s.at[k], ret_r.at[k], yz - k)
        c.start()
        back_copies.append(c)
    sent += back_copies
    for c in back_copies:
        c.wait_recv()
    for b in range(blocks):
        total = jnp.where(dest[b] == me, back[0], jnp.zeros((8, block), f32))
        for k in range(1, yz):
            total = total + jnp.where(dest[b] == peer(k), came[k], jnp.zeros((8, block), f32))
        out[:, b * block : (b + 1) * block] = total
    for c in sent:
        c.wait_send()


def on_device(
    positions,
    species,
    features,
    move_dest,
    move_slot,
    halo_list,
    neighbours,
    neighbour_count,
    wave_index,
    radial_in,
    radial_mid,
    radial_out,
    up_weight,
    prod_weight,
    out_weight,
    skip_weight,
    charge_weight,
    field_weight,
    read_weight,
    read_vector,
    force_weight,
):
    gx, yz = lax.axis_size("gx"), lax.axis_size("yz")
    atoms, width = features.shape
    block = atoms // move_dest.shape[0]
    slots = neighbours.shape[1]
    channels = width // 4
    latent = charge_weight.shape[1]
    nyp = -(-(2 * yz + 1) // 8) * 8
    pairs = 2 * gx * (2 * z_reach + 1)
    share = pairs * latent // yz
    wide = -(-4 * nyp // lanes) * lanes
    halo = halo_list.shape[0]
    groups = slots // group
    table = atoms + 4 * halo
    hidden = radial_mid.shape[1]

    def dma(n):
        return [pltpu.SemaphoreType.DMA((n,)), pltpu.SemaphoreType.DMA((n,))]

    scratch = [
        pltpu.VMEM((8, atoms), f32),
        pltpu.VMEM((yz, 8, block), f32),
        pltpu.VMEM((yz, 8, block), f32),
        pltpu.VMEM((yz, block, width), bf16),
        pltpu.VMEM((yz, block, width), bf16),
        pltpu.VMEM((atoms, width), bf16),
        pltpu.VMEM((8, 4 * halo), f32),
        pltpu.VMEM((4, 8, 4 * halo), f32),
        pltpu.VMEM((halo, width), bf16),
        pltpu.VMEM((4, halo, width), bf16),
        pltpu.VMEM((2, pairs, atoms), f32),
        pltpu.VMEM((wide, 2 * atoms), f32),
        pltpu.VMEM((wide, 2 * atoms), f32),
        pltpu.VMEM((yz, share, wide), f32),
        pltpu.VMEM((yz, share, wide), f32),
        pltpu.VMEM((share, wide), f32),
        pltpu.VMEM((gx, share, wide), f32),
        pltpu.VMEM((share, wide), f32),
        pltpu.VMEM((yz, share, wide), f32),
        pltpu.VMEM((groups, group, atoms), i32),
        pltpu.VMEM((groups, 3, group, atoms), f32),
        pltpu.VMEM((groups, group, hidden, atoms), bf16),
        pltpu.VMEM((width, table), bf16),
        pltpu.VMEM((4, channels, atoms), f32),
        pltpu.VMEM((yz, 8, block), f32),
        pltpu.VMEM((yz, 8, block), f32),
    ]
    scratch += dma(yz) + dma(yz) + dma(4) + dma(4) + dma(yz) + dma(gx) + dma(yz) + dma(yz)
    out = pl.pallas_call(
        functools.partial(step_kernel, (gx, yz, nyp)),
        out_shape=jax.ShapeDtypeStruct((8, atoms), f32),
        in_specs=[SMEM, SMEM] + [VMEM] * 19,
        out_specs=VMEM,
        scratch_shapes=scratch,
        compiler_params=pltpu.CompilerParams(
            collective_id=0, has_side_effects=True, vmem_limit_bytes=56 * 1024 * 1024
        ),
    )(
        move_dest,
        move_slot,
        positions,
        species.reshape(1, atoms),
        features,
        halo_list.reshape(1, halo),
        neighbours,
        neighbour_count.reshape(1, atoms),
        wave_index,
        radial_in,
        radial_mid,
        radial_out,
        up_weight,
        prod_weight,
        out_weight,
        skip_weight,
        charge_weight,
        field_weight,
        read_weight,
        read_vector.reshape(1, -1),
        force_weight.reshape(1, -1),
    )
    return out[:3], out[3]


def solution(mesh):
    split = P(("gx", "yz"))
    rows = P(("gx", "yz"), None)
    in_specs = (P(None, ("gx", "yz")), split, rows, split, split, split, rows, split) + (P(),) * 13
    out_specs = (P(None, ("gx", "yz")), split)
    return jax.shard_map(
        on_device, mesh=mesh, in_specs=in_specs, out_specs=out_specs, check_vma=False
    )
```

time: 121 us -> 61 us (0.50)
  blocking collectives: 36.6 us -> 0 us
  starting transfers between devices: 11.8 us -> 0 us
  waiting for transfers between devices: 11.5 us -> 0 us
  Pallas kernels: 48.9 us -> 54 us
  local copies, waits for them, and re-layouts: 9.67 us -> 6.13 us
    all_gather x2 -> x0, blocking collectives: 27.8 us -> none  [the longest x1 16.5 us: on_device(): row_sums = jnp.sum(lax.all_gather(partial, 'gx'), axis=0)]
    all_to_all x1 -> x0, waiting for transfers between devices: 11.5 us -> none  [on_device(): lax.all_to_all(outgoing, 'yz', split_axis=0, concat_axis=0, tiled=True)]
    all_to_all x1 -> x0, blocking collectives: 8.77 us -> none  [on_device(): came = lax.all_to_all(back, 'yz', split_axis=0, concat_axis=0, tiled=True)]
    ppermute x4 -> x0, starting transfers between devices: 6.47 us -> none  [ring(): lax.ppermute(send, axis, [(i, (i + step) % count) for i in range(count)])]
    all_to_all x1 -> x0, starting transfers between devices: 5.34 us -> none  [on_device(): lax.all_to_all(outgoing, 'yz', split_axis=0, concat_axis=0, tiled=True)]
    pallas_call x8 -> x1, Pallas kernels: 48.9 us -> 54 us  [on_device(): pl.pallas_call(functools.partial(step_kernel, (gx, yz, nyp)), out_shape=j...]
    reshape x5 -> x0, local copies, waits for them, and re-layouts: 2.83 us -> none  [the longest x1 0.76 us: on_device(): neighbours.reshape(steps, 1, edges)]
    slice x1 -> x2, local copies, waits for them, and re-layouts: 1.47 us -> 2.55 us  [on_device(): return (out[:3], out[3])]
  transfers between devices with their start and end apart: 5 -> 0, of which waited for: 1 -> 0; matrix products, arithmetic and copies ran while one was open for 6% -> 0% of each run, Pallas kernels for 4% -> 0%
where the time goes in v1:
time: 61 us; the launch traced here: 60.7 us
  Pallas kernels  54 us (89%)
  local copies, waits for them, and re-layouts  6.13 us (10%)
  between operations  0.65 us (1%)
    pallas_call x1, Pallas kernels, on_device(): pl.pallas_call(functools.partial(step_kernel, (gx, yz, nyp)), out_shape=j...  54 us
    unnamed x5, local copies, waits for them, and re-layouts  3.58 us
    slice x2, local copies, waits for them, and re-layouts, on_device(): return (out[:3], out[3])  2.55 us

profile of v1, /device:TPU:0, one launch (start us, length us, event | category | flops | bytes accessed | tf_op | source)
XLA Modules:
  0.0 60.7 jit_solution(18268041304586213982)
XLA Ops:
  0.6 0.0 copy-start
  0.6 1.4 %copy.24.charge = bf16[128,8]{1,0:T(8,128)(2,1)} copy(bf16[128,8]{0,1:T(8,128)(2,1)} %param.37) | data formatting | bytes 4096 | tf_op args[16]
  2.1 1.4 %copy.25.readw = bf16[128,16]{1,0:T(8,128)(2,1)} copy(bf16[128,16]{0,1:T(8,128)(2,1)} %param.39) | data formatting | bytes 8192 | tf_op args[18]
  3.5 0.0 copy-done
  3.5 0.8 %copy.23.nbr = s32[256,64]{1,0:T(8,128)} copy(s32[256,64]{0,1:T(8,128)S(1)} %copy-done) | data formatting | bytes 131072 | tf_op args[6]
  4.2 54.0 %shard_map.212 = f32[8,256]{1,0:T(8,128)} custom-call(s32[2]{0:T(128)} %dest.1, s32[2]{0:T(128)} %slot.1, bf16[3,256]{1,0:T(4,128)(2,1)} %pos.1, s32[1,256]{1,0:T(1,128)} %bitcast.6, bf16[256,512]{1,0:T(8,128)(2,1)} %feat.1, s32[1,32]{1,0:T(1,128)} %bitcast.9, s32[256,64]{1,0:T(8,128)} %copy.23.nbr, s32[1,256]{1,0:T(1,128)} %bitcast.7, s32[3,4096]{1,0:T(4,128)} %wave.1, ...), custom_call_target="tpu_custom_call" | custom-call | tf_op jit(solution)/shard_map/pallas_call | solution.py:519
  58.2 1.3 %slice.7 = f32[1,256]{1,0:T(1,128)} slice(f32[8,256]{1,0:T(8,128)} %shard_map.212), slice={[3:4], [0:256]} | slice | bytes 2048 | tf_op jit(solution)/shard_map/slice | solution.py:551
  59.5 1.3 %slice.6 = f32[3,256]{1,0:T(4,128)} slice(f32[8,256]{1,0:T(8,128)} %shard_map.212), slice={[0:3], [0:256]} | slice | bytes 6144 | tf_op jit(solution)/shard_map/slice | solution.py:551
Async XLA Ops:
  0.6 2.8 %copy-start = (s32[256,64]{0,1:T(8,128)S(1)}, s32[256,64]{0,1:T(8,128)}, u32[]{:S(2)}) copy-start(s32[256,64]{0,1:T(8,128)} %param.27) | copy-start | bytes 196612

commit v2 on v1

v2 whole, which is shorter than its diff:
```python
import functools
import math

import jax
import jax.numpy as jnp
from jax import lax
from jax.experimental import pallas as pl
from jax.experimental.pallas import tpu as pltpu
from jax.sharding import PartitionSpec as P

highest = lax.Precision.HIGHEST
two_pi = 2.0 * math.pi
cutoff_radius = 3.5
basis_sharpness = 4.0
ewald_width = 0.1
ewald_scale = 0.01
z_reach = 2
lanes = 128
group = 8
f32 = jnp.float32
bf16 = jnp.bfloat16
i32 = jnp.int32

VMEM = pl.BlockSpec(memory_space=pltpu.VMEM)
MESH = pl.DeviceIdType.MESH
NT = (((1,), (1,)), ((), ()))
TN = (((0,), (0,)), ((), ()))


def nt(a, b, precision=None):
    return lax.dot_general(a, b, NT, precision=precision, preferred_element_type=f32)


def tn(a, b, precision=None):
    return lax.dot_general(a, b, TN, precision=precision, preferred_element_type=f32)


def mm(a, b, precision=None):
    return jnp.dot(a, b, precision=precision, preferred_element_type=f32)


def iota(shape, dim):
    return lax.broadcasted_iota(jnp.int32, shape, dim)


def silu(v):
    half = 0.5 * v
    return half + half * jnp.tanh(half)


def turn_cos_sin(turns):
    frac = turns - jnp.floor(turns + 0.5)
    angle = two_pi * frac
    return jnp.cos(angle), jnp.sin(angle)


def flip(a):
    return a.astype(f32).T.astype(a.dtype)


def split(a):
    high = a.astype(bf16)
    return high, (a - high.astype(f32)).astype(bf16)


fields = (
    "dest", "slot", "pos", "species", "feat", "halo", "wave", "nbr", "count", "rin", "mid",
    "rout", "up", "prod", "ow", "sw", "charge", "fieldw", "readw", "rvec", "fw",
)


def step_kernel(sizes, *refs):
    gx, yz, nyp = sizes
    n_in = len(fields)
    sources, refs = refs[:n_in], refs[n_in:]
    forces, energies = refs[:2]
    local, refs = dict(zip(fields, refs[2 : 2 + n_in])), refs[2 + n_in :]
    (
        meta_in, meta_got, spread, pieces, work, halo_pos, ghost_pos, halo_feat, ghost_feat,
        xz, ymat, ypair, part_out, part_got, row_sum, row_got, coef, coefs,
        rel, hidden, radials, table_t, acc, back, came,
        in_s, meta_s, meta_r, sp_s, sp_r, pc_s, pc_r, hp_s, hp_r, hf_s, hf_r, rs_s, rs_r,
        gs_s, gs_r, ag_s, ag_r, ret_s, ret_r,
    ) = refs
    row, me = lax.axis_index("gx"), lax.axis_index("yz")
    blocks, parts, piece, width = local["feat"].shape
    channels = width // 4
    block = parts * piece
    atoms = blocks * block
    slots = local["nbr"].shape[0]
    groups = slots // group
    latent = local["charge"].shape[0]
    nx = 2 * gx
    pairs = nx * (2 * z_reach + 1)
    share = pairs * latent // yz
    halos = local["halo"].shape[1]
    width_y = ymat.shape[0]

    def peer(k):
        return lax.rem(me + k, yz)

    def row_peer(k):
        return lax.rem(row + k, gx)

    def to_yz(src, dst, s, r, k):
        return pltpu.make_async_remote_copy(
            src_ref=src, dst_ref=dst, send_sem=s, recv_sem=r,
            device_id={"yz": peer(k)}, device_id_type=MESH,
        )

    def to_gx(src, dst, s, r, k):
        return pltpu.make_async_remote_copy(
            src_ref=src, dst_ref=dst, send_sem=s, recv_sem=r,
            device_id={"gx": row_peer(k)}, device_id_type=MESH,
        )

    barrier = pltpu.get_barrier_semaphore()
    for k in range(1, yz):
        pl.semaphore_signal(barrier, inc=1, device_id={"yz": peer(k)}, device_id_type=MESH)
    for k in range(1, gx):
        pl.semaphore_signal(barrier, inc=1, device_id={"gx": row_peer(k)}, device_id_type=MESH)
    loads = {}
    for i, name in enumerate(fields):
        loads[name] = pltpu.make_async_copy(sources[i], local[name], in_s.at[i])
        loads[name].start()

    def use(name):
        if name in loads:
            loads.pop(name).wait()
        return local[name]

    dest, slot = use("dest"), use("slot")
    lane = iota((1, atoms), 1)
    place = jnp.zeros((1, atoms), i32)
    spot = jnp.zeros((1, atoms), i32)
    for b in range(blocks):
        code = dest[:, b : b + 1] * blocks + slot[:, b : b + 1]
        place = jnp.where(lane // block == b, code, place)
        spot = jnp.where(lane // piece == me * blocks + b, code * piece + lane % piece, spot)
    meta_in[...] = jnp.concatenate(
        [
            use("pos")[...].astype(f32),
            use("species")[...].astype(f32),
            place.astype(f32),
            spot.astype(f32),
            jnp.zeros((2, atoms), f32),
        ],
        axis=0,
    )
    feat = use("feat")
    pl.semaphore_wait(barrier, yz - 1 + gx - 1)

    sent = []

    def start(copies):
        for c in copies:
            c.start()
        sent.extend(copies)
        return copies

    def arrive(copies):
        for c in copies:
            c.wait_recv()

    others = range(1, yz)
    meta_copies = start(
        [to_yz(meta_in, meta_got.at[k], meta_s.at[k], meta_r.at[k], k) for k in others]
    )
    spread_copies = start(
        [to_yz(feat.at[:, peer(k)], spread.at[me], sp_s.at[k], sp_r.at[k], k) for k in others]
    )

    spread[me] = feat[:, pl.ds(me, 1)].reshape(blocks, piece, width)
    meta_got[0] = meta_in[...]
    wave = use("wave")
    codes = (wave[2:3, :] + z_reach) * nx + wave[0:1, :] - 1
    waves = wave.shape[1]
    hot = ((me * share + iota((share, waves), 0)) // latent == codes).astype(f32).astype(bf16)
    level = iota((nyp, waves), 0)
    plus = (level == wave[1:2, :]).astype(f32).astype(bf16)
    minus = ((level == -wave[1:2, :]) & (level > 0)).astype(f32).astype(bf16)
    pair = (me * share + iota((share, nyp), 0)) // latent
    wx = ((pair % nx) + 1).astype(f32) * (two_pi / gx)
    wz = ((pair // nx) - z_reach).astype(f32) * two_pi
    wy = iota((share, nyp), 1).astype(f32) * (two_pi / yz)
    squared = wx * wx + wy * wy + wz * wz
    prefactor = 8.0 * math.pi * ewald_scale / (gx * yz)
    weight = prefactor * jnp.exp(-0.5 * ewald_width * ewald_width * squared) / squared
    gp, gm = weight * nt(hot, plus), weight * nt(hot, minus)
    rin = use("rin")
    rin_t = jnp.concatenate([rin[...].astype(f32), jnp.zeros_like(rin, f32)], axis=0).T.astype(bf16)
    mid = use("mid")
    mid_t = [flip(mid[i]) for i in range(2)]
    rout_t = flip(use("rout")[...])
    list4 = jnp.concatenate([use("halo")[...]] * 4, axis=1)
    pick_t = (iota((atoms, 4 * halos), 0) == list4).astype(f32)
    pick = pick_t.T[:halos].astype(bf16)
    force8 = jnp.broadcast_to(use("fw")[...], (8, channels))
    ow, sw = use("ow"), use("sw")
    to_b = nt(force8, ow[1].astype(f32), highest)
    to_f = nt(force8, sw[1].astype(f32), highest)
    nbr, counts = use("nbr"), use("count")[...]

    arrive(meta_copies)
    metas = []
    for s in range(blocks):
        mine = (me * blocks + s).astype(f32)
        total = jnp.zeros((8, block), f32)
        for k in range(yz):
            for b in range(blocks):
                got = meta_got[k, :, b * block : (b + 1) * block]
                total = total + jnp.where(got[4:5, :] == mine, got, 0.0)
        metas.append(total)
    meta = jnp.concatenate(metas, axis=1)
    halo_pos[...] = mm(meta.astype(bf16), pick_t.astype(bf16))
    ways = ((to_gx, 1), (to_gx, gx - 1), (to_yz, 1), (to_yz, yz - 1))
    ghost_copies = start(
        [send(halo_pos, ghost_pos.at[i], hp_s.at[i], hp_r.at[i], k) for i, (send, k) in enumerate(ways)]
    )
    targets = meta_got[0, 5:6, :]
    for k in range(1, yz):
        targets = targets + meta_got[k, 5:6, :]
    route = (iota((atoms, atoms), 0).astype(f32) == targets).astype(f32).astype(bf16)

    x_turns = (meta[0:1] + row.astype(f32)) * (1.0 / gx)
    y_turns = (meta[1:2] + me.astype(f32)) * (1.0 / yz)
    xc, xs = turn_cos_sin((iota((nx, atoms), 0) + 1).astype(f32) * x_turns)
    zc, zs = turn_cos_sin((iota((8, atoms), 0) - z_reach).astype(f32) * meta[2:3])
    yc, ys = turn_cos_sin(iota((nyp, atoms), 0).astype(f32) * y_turns)
    for m in range(2 * z_reach + 1):
        c1, s1 = zc[m : m + 1], zs[m : m + 1]
        xz[0, m * nx : (m + 1) * nx, :] = xc * c1 - xs * s1
        xz[1, m * nx : (m + 1) * nx, :] = xc * s1 + xs * c1
    ymat[...] = jnp.zeros_like(ymat)
    rise = iota((nyp, atoms), 0).astype(f32) * (two_pi / yz)
    for half in range(2):
        cut = slice(half * atoms, (half + 1) * atoms)
        far = slice((2 + half) * atoms, (3 + half) * atoms)
        sign = -1.0 if half == 0 else 1.0
        base = 2 * half * nyp
        ymat[base : base + nyp, cut] = yc
        ymat[base + nyp : base + 2 * nyp, cut] = ys
        ymat[base : base + nyp, far] = sign * rise * ys
        ymat[base + nyp : base + 2 * nyp, far] = -sign * rise * yc
    high, low = split(ymat[...])
    ypair[:width_y, :] = high
    ypair[width_y:, :] = low

    arrive(spread_copies)
    pieces[...] = (
        mm(route, spread[...].reshape(atoms, width)).astype(bf16).reshape(yz, blocks, piece, width)
    )
    piece_copies = start(
        [to_yz(pieces.at[peer(k)], work.at[:, me], pc_s.at[k], pc_r.at[k], k) for k in others]
    )
    work[:, pl.ds(me, 1)] = pieces[me].reshape(blocks, 1, piece, width)

    arrive(ghost_copies)
    part = iota((8, 4 * halos), 1) // halos
    lead = iota((8, 4 * halos), 0)
    ghosts = jnp.zeros((8, 4 * halos), f32)
    for i, (axis, shift) in enumerate(((0, -1.0), (0, 1.0), (1, -1.0), (1, 1.0))):
        ghosts = jnp.where(part == i, ghost_pos[i] + jnp.where(lead == axis, shift, 0.0), ghosts)
    table_pos = jnp.concatenate([meta, ghosts], axis=1)
    table = table_pos.shape[1]
    nrad = rin.shape[0]
    centres = iota((2 * nrad, atoms), 0).astype(f32) * (cutoff_radius / (nrad - 1))

    def radial_step(g, carry):
        index = nbr[pl.ds(pl.multiple_of(g * group, group), group), :]
        local_index = index % lanes
        where = index // lanes
        rs = []
        for m in range(3):
            cols = []
            for h in range(atoms // lanes):
                cut = slice(h * lanes, (h + 1) * lanes)
                found = jnp.zeros((group, lanes), f32)
                for t in range(table // lanes):
                    tile = jnp.broadcast_to(
                        table_pos[m : m + 1, t * lanes : (t + 1) * lanes], (group, lanes)
                    )
                    got = jnp.take_along_axis(
                        tile, local_index[:, cut], axis=1, mode="promise_in_bounds"
                    )
                    found = jnp.where(where[:, cut] == t, got, found)
                cols.append(found)
            r = jnp.concatenate(cols, axis=1) - meta[m : m + 1]
            rel[g, m] = r
            rs.append(r)
        dist = jnp.sqrt(rs[0] * rs[0] + rs[1] * rs[1] + rs[2] * rs[2])
        u = dist * (1.0 / cutoff_radius)
        u2 = u * u
        u6 = u2 * u2 * u2
        env = 1.0 + u6 * (-28.0 + u * (48.0 - 21.0 * u))
        live = (iota((group, atoms), 0) + g * group) < counts
        env = jnp.where(live, env, 0.0)
        basis = []
        for s in range(group):
            off = dist[s : s + 1] - centres
            basis.append(jnp.exp(-basis_sharpness * off * off))
        h = silu(mm(rin_t, jnp.concatenate(basis, axis=1).astype(bf16))).astype(bf16)
        h = silu(mm(mid_t[0], h)).astype(bf16)
        h = silu(mm(mid_t[1], h))
        for s in range(group):
            hidden[g, s] = (h[:, s * atoms : (s + 1) * atoms] * env[s : s + 1]).astype(bf16)
        return carry

    lax.fori_loop(0, groups, radial_step, 0)

    arrive(piece_copies)
    owned = work[...].reshape(atoms, width)
    halo_feat[...] = mm(pick, owned).astype(bf16)
    halo_copies = start(
        [send(halo_feat, ghost_feat.at[i], hf_s.at[i], hf_r.at[i], k) for i, (send, k) in enumerate(ways)]
    )

    scalars = owned[:, :channels]
    q = nt(use("charge")[...], scalars)
    weighted = [
        (xz[i][:, None, :] * q[None]).reshape(pairs * latent, atoms) for i in range(2)
    ]
    high, low = split(jnp.concatenate(weighted, axis=1))
    cut = slice(0, 2 * atoms)
    wide = nt(high, ypair[:, cut])
    part_out[...] = (
        wide[:, :width_y] + wide[:, width_y:] + nt(low, ypair[:width_y, cut])
    ).reshape(yz, share, width_y)
    part_copies = start(
        [to_yz(part_out.at[peer(k)], part_got.at[k], rs_s.at[k], rs_r.at[k], k) for k in others]
    )

    up = use("up")

    def raise_rows(rows, begin, size):
        for p in range(4):
            cut = slice(p * channels, (p + 1) * channels)
            got = mm(rows[:, cut], up[min(p, 1)])
            table_t[cut, begin : begin + size] = got.T.astype(bf16)

    raise_rows(owned, 0, atoms)

    skip = mm(scalars, sw[0]).T
    pulls = [
        nt(to_f, owned[:, (1 + m) * channels : (2 + m) * channels].astype(f32), highest)[0:1]
        for m in range(3)
    ]
    prod = use("prod")
    kinds = prod.shape[0]
    which = (iota((8, atoms), 0).astype(f32) == meta[3:4]).astype(f32).astype(bf16)
    weights = prod[...]
    high = weights.astype(bf16).astype(f32)
    middle = (weights - high).astype(bf16).astype(f32)
    low = weights - high - middle
    blank = jnp.zeros((8 - kinds, weights.shape[1]), f32)
    stack = jnp.concatenate([high, blank, middle, blank, low, blank], axis=0)
    p_t = tn(stack.astype(bf16), jnp.concatenate([which] * 3, axis=0))

    def spread_step(g, carry):
        for s in range(group):
            radials[g, s] = mm(rout_t, hidden[g, s]).astype(bf16)
        return carry

    lax.fori_loop(0, groups, spread_step, 0)
    acc[...] = jnp.zeros_like(acc)
    arrive(halo_copies)
    raise_rows(jnp.concatenate([ghost_feat[i] for i in range(4)], axis=0), atoms, 4 * halos)

    def message_step(g, carry):
        index = nbr[pl.ds(pl.multiple_of(g * group, group), group), :]
        r = [rel[g, m] for m in range(3)]
        for s in range(group):
            hot_t = (iota((table, atoms), 0) == index[s : s + 1]).astype(f32).astype(bf16)
            u = mm(table_t[...], hot_t)
            us = [u[p * channels : (p + 1) * channels] for p in range(4)]
            rads = [
                radials[g, s, p * channels : (p + 1) * channels, :].astype(f32) for p in range(4)
            ]
            rm = [r[m][s : s + 1] for m in range(3)]
            along = rm[0] * us[1] + rm[1] * us[2] + rm[2] * us[3]
            acc[0] += rads[0] * us[0] + rads[1] * along
            ru = rads[2] * us[0]
            for m in range(3):
                acc[1 + m] += ru * rm[m] + rads[3] * us[1 + m]
        return carry

    first, second = groups // 4, 5 * groups // 8
    lax.fori_loop(0, first, message_step, 0)

    arrive(part_copies)
    total = part_out[me]
    for k in range(1, yz):
        total = total + part_got[k]
    row_sum[...] = total
    row_copies = start(
        [to_gx(row_sum, row_got.at[k], gs_s.at[k], gs_r.at[k], k) for k in range(1, gx)]
    )

    lax.fori_loop(first, second, message_step, 0)

    arrive(row_copies)
    total = row_sum[...]
    for k in range(1, gx):
        total = total + row_got[k]
    quarters = [total[:, i * nyp : (i + 1) * nyp] for i in range(4)]
    rest = jnp.zeros((share, width_y - 4 * nyp), f32)
    both, gap = gp + gm, gp - gm
    coef[...] = jnp.concatenate(
        [
            both * quarters[0] - gap * quarters[3],
            both * quarters[1] + gap * quarters[2],
            both * quarters[2] + gap * quarters[1],
            both * quarters[3] - gap * quarters[0],
            rest,
        ],
        axis=1,
    )
    coef_copies = start(
        [to_yz(coef, coefs.at[me], ag_s.at[k], ag_r.at[k], k) for k in others]
    )
    coefs[me] = coef[...]

    lax.fori_loop(second, groups, message_step, 0)

    arrive(coef_copies)
    high, low = split(coefs[...].reshape(yz * share, width_y))
    v = mm(jnp.concatenate([high, high], axis=1), ypair[...]) + mm(low, ypair[:width_y, :])
    v_re, v_im, y_im, y_re = [v[:, i * atoms : (i + 1) * atoms] for i in range(4)]
    zero = jnp.zeros((latent, atoms), f32)
    potential, field = zero, [zero, zero, zero]
    for j in range(pairs):
        cut = slice(j * latent, (j + 1) * latent)
        cos_row, sin_row = xz[0, j : j + 1], xz[1, j : j + 1]
        d_im = cos_row * v_im[cut] - sin_row * v_re[cut]
        potential = potential + (cos_row * v_re[cut] + sin_row * v_im[cut])
        field[0] = field[0] - ((j % nx) + 1) * (two_pi / gx) * d_im
        field[1] = field[1] - (cos_row * y_im[cut] - sin_row * y_re[cut])
        field[2] = field[2] - ((j // nx) - z_reach) * two_pi * d_im

    scale = 1.0 / math.sqrt(slots)
    p = [p_t[i * channels : (i + 1) * channels] for i in range(5)]
    a0 = acc[0] * scale
    a1 = [acc[1 + m] * scale for m in range(3)]
    square = a1[0] * a1[0] + a1[1] * a1[1] + a1[2] * a1[2]
    b0 = (p[0] * a0 + p[1] * a0 * a0 + p[2] * square).astype(bf16)
    b1 = [(p[3] * a1[m] + p[4] * a0 * a1[m]).astype(bf16) for m in range(3)]
    scal = tn(ow[0], b0) + skip + tn(use("fieldw")[...], potential, highest)
    readout = silu(mm(use("readw")[...], scal.astype(bf16)))
    rvec = use("rvec")
    tall = jnp.broadcast_to(rvec[...], (8, rvec.shape[1]))
    energy = mm(tall, readout, highest)[0:1] + 0.5 * jnp.sum(q * potential, axis=0, keepdims=True)
    rows = []
    for m in range(3):
        rows.append(
            mm(to_b, b1[m].astype(f32), highest)[0:1]
            + pulls[m]
            + jnp.sum(q * field[m], axis=0, keepdims=True)
        )
    result = jnp.concatenate(rows + [energy, jnp.zeros((4, atoms), f32)], axis=0)
    for k in range(yz):
        for b in range(blocks):
            cut = slice(b * block, (b + 1) * block)
            code = meta_got[k, 4:5, cut]
            total = jnp.zeros((8, block), f32)
            for s in range(blocks):
                mine = (me * blocks + s).astype(f32)
                total = total + jnp.where(
                    code == mine, result[:, s * block : (s + 1) * block], 0.0
                )
            back[k, :, cut] = total
    back_copies = start(
        [to_yz(back.at[k], came.at[k], ret_s.at[k], ret_r.at[k], yz - k) for k in others]
    )
    arrive(back_copies)
    total = back[0]
    for k in range(1, yz):
        total = total + came[k]
    forces[...] = total[:3]
    energies[...] = total[3:4]
    for c in sent:
        c.wait_send()
    assert not loads


def on_device(
    positions,
    species,
    features,
    move_dest,
    move_slot,
    halo_list,
    neighbours,
    neighbour_count,
    wave_index,
    radial_in,
    radial_mid,
    radial_out,
    up_weight,
    prod_weight,
    out_weight,
    skip_weight,
    charge_weight,
    field_weight,
    read_weight,
    read_vector,
    force_weight,
):
    gx, yz = lax.axis_size("gx"), lax.axis_size("yz")
    atoms, width = features.shape
    blocks = move_dest.shape[0]
    piece = atoms // blocks // yz
    slots = neighbours.shape[1]
    channels = width // 4
    latent = charge_weight.shape[1]
    nyp = -(-(2 * yz + 1) // 8) * 8
    pairs = 2 * gx * (2 * z_reach + 1)
    share = pairs * latent // yz
    wide = -(-4 * nyp // lanes) * lanes
    halo = halo_list.shape[0]
    groups = slots // group
    table = atoms + 4 * halo
    hidden = radial_mid.shape[1]

    given = {
        "dest": move_dest.reshape(1, -1),
        "slot": move_slot.reshape(1, -1),
        "pos": positions,
        "species": species.reshape(1, -1),
        "feat": features.reshape(blocks, yz, piece, width),
        "halo": halo_list.reshape(1, -1),
        "wave": wave_index,
        "nbr": neighbours.T,
        "count": neighbour_count.reshape(1, -1),
        "rin": radial_in,
        "mid": radial_mid,
        "rout": radial_out,
        "up": up_weight,
        "prod": prod_weight,
        "ow": out_weight,
        "sw": skip_weight,
        "charge": charge_weight.T,
        "fieldw": field_weight,
        "readw": read_weight.T,
        "rvec": read_vector.reshape(1, -1),
        "fw": force_weight.reshape(1, -1),
    }

    def dma(n):
        return [pltpu.SemaphoreType.DMA((n,)), pltpu.SemaphoreType.DMA((n,))]

    scratch = [pltpu.VMEM(given[name].shape, given[name].dtype) for name in fields]
    scratch += [
        pltpu.VMEM((8, atoms), f32),
        pltpu.VMEM((yz, 8, atoms), f32),
        pltpu.VMEM((yz, blocks, piece, width), bf16),
        pltpu.VMEM((yz, blocks, piece, width), bf16),
        pltpu.VMEM((blocks, yz, piece, width), bf16),
        pltpu.VMEM((8, 4 * halo), f32),
        pltpu.VMEM((4, 8, 4 * halo), f32),
        pltpu.VMEM((halo, width), bf16),
        pltpu.VMEM((4, halo, width), bf16),
        pltpu.VMEM((2, pairs, atoms), f32),
        pltpu.VMEM((wide, 4 * atoms), f32),
        pltpu.VMEM((2 * wide, 4 * atoms), bf16),
        pltpu.VMEM((yz, share, wide), f32),
        pltpu.VMEM((yz, share, wide), f32),
        pltpu.VMEM((share, wide), f32),
        pltpu.VMEM((gx, share, wide), f32),
        pltpu.VMEM((share, wide), f32),
        pltpu.VMEM((yz, share, wide), f32),
        pltpu.VMEM((groups, 3, group, atoms), f32),
        pltpu.VMEM((groups, group, hidden, atoms), bf16),
        pltpu.VMEM((groups, group, width, atoms), bf16),
        pltpu.VMEM((width, table), bf16),
        pltpu.VMEM((4, channels, atoms), f32),
        pltpu.VMEM((yz, 8, atoms), f32),
        pltpu.VMEM((yz, 8, atoms), f32),
    ]
    scratch += [pltpu.SemaphoreType.DMA((len(fields),))]
    scratch += dma(yz) + dma(yz) + dma(yz) + dma(4) + dma(4) + dma(yz) + dma(gx) + dma(yz) + dma(yz)
    forces, energies = pl.pallas_call(
        functools.partial(step_kernel, (gx, yz, nyp)),
        out_shape=[
            jax.ShapeDtypeStruct((3, atoms), f32),
            jax.ShapeDtypeStruct((1, atoms), f32),
        ],
        in_specs=[pl.BlockSpec(memory_space=pl.ANY)] * len(fields),
        out_specs=[VMEM, VMEM],
        scratch_shapes=scratch,
        compiler_params=pltpu.CompilerParams(
            collective_id=0, has_side_effects=True, vmem_limit_bytes=56 * 1024 * 1024
        ),
    )(*[given[name] for name in fields])
    return forces, energies.reshape(atoms)


def solution(mesh):
    split = P(("gx", "yz"))
    rows = P(("gx", "yz"), None)
    in_specs = (P(None, ("gx", "yz")), split, rows, split, split, split, rows, split) + (P(),) * 13
    out_specs = (P(None, ("gx", "yz")), split)
    return jax.shard_map(
        on_device, mesh=mesh, in_specs=in_specs, out_specs=out_specs, check_vma=False
    )
```

time: 61 us -> 50.4 us (0.83)
  Pallas kernels: 54 us -> 47.7 us
  local copies, waits for them, and re-layouts: 6.13 us -> 1.87 us
    pallas_call x1, Pallas kernels: 54 us -> 47.7 us  [on_device(): pl.pallas_call(functools.partial(step_kernel, (gx, yz, nyp)), out_shape=[...]
    slice x2 -> x0, local copies, waits for them, and re-layouts: 2.55 us -> none  [on_device(): return (out[:3], out[3])]
    unnamed x5 -> x6, local copies, waits for them, and re-layouts: 3.58 us -> 1.87 us
where the time goes in v2:
time: 50.4 us; the launch traced here: 50.2 us
  Pallas kernels  47.7 us (95%)
  local copies, waits for them, and re-layouts  1.87 us (4%)
  between operations  0.66 us (1%)
    pallas_call x1, Pallas kernels, on_device(): pl.pallas_call(functools.partial(step_kernel, (gx, yz, nyp)), out_shape=[...  47.7 us
    unnamed x6, local copies, waits for them, and re-layouts  1.87 us

profile of v2, /device:TPU:0, one launch (start us, length us, event | category | flops | bytes accessed | tf_op | source)
XLA Modules:
  0.0 50.2 jit_solution(16601455061811177070)
XLA Ops:
  0.6 47.7 %shard_map.212 = (f32[3,256]{1,0:T(4,128)}, f32[1,256]{1,0:T(1,128)}) custom-call(s32[1,2]{1,0:T(1,128)} %bitcast.19, s32[1,2]{1,0:T(1,128)} %bitcast.20, bf16[3,256]{1,0:T(4,128)(2,1)} %refs_2_.1, s32[1,256]{1,0:T(1,128)} %bitcast.16, bf16[2,8,16,512]{3,2,1,0:T(8,128)(2,1)} %bitcast.12, s32[1,32]{1,0:T(1,128)} %bitcast.21, s32[3,4096]{1,0:T(4,128)} %refs_6_.1, ...), custom_call_target="tpu_custom_call" | custom-call | tf_op jit(solution)/shard_map/pallas_call | solution.py:581
  48.3 0.0 copy-start
  48.3 0.7 %copy-done = f32[3,256]{1,0:T(4,128)S(1)} copy-done((f32[3,256]{1,0:T(4,128)S(1)}, f32[3,256]{1,0:T(4,128)}, u32[]{:S(2)}) %copy-start) | copy-done | bytes 3096
  49.0 0.0 copy-start.1
  49.0 0.6 %copy.25 = f32[3,256]{1,0:T(4,128)} copy(f32[3,256]{1,0:T(4,128)S(1)} %copy-done) | data formatting | bytes 6144
  49.6 0.0 copy-done.1
  49.6 0.6 %copy.26 = f32[256]{0:T(256)} copy(f32[256]{0:T(256)S(1)} %bitcast.18) | data formatting | bytes 2048
Async XLA Ops:
  48.3 0.7 %copy-start = (f32[3,256]{1,0:T(4,128)S(1)}, f32[3,256]{1,0:T(4,128)}, u32[]{:S(2)}) copy-start(f32[3,256]{1,0:T(4,128)} %get-tuple-element.8) | copy-start | bytes 9220
  49.0 0.6 %copy-start.1 = (f32[1,256]{1,0:T(1,128)S(1)}, f32[1,256]{1,0:T(1,128)}, u32[]{:S(2)}) copy-start(f32[1,256]{1,0:T(1,128)} %get-tuple-element.5) | copy-start | bytes 3076

commit v3 on v2

--- a/solution.py
+++ b/solution.py
@@ -17,6 +17,7 @@
 z_reach = 2
 lanes = 128
 group = 8
+together = 2
 f32 = jnp.float32
 bf16 = jnp.bfloat16
 i32 = jnp.int32
@@ -63,6 +64,11 @@
     return high, (a - high.astype(f32)).astype(bf16)
 
 
+def interleave(parts):
+    tall = parts[0].shape[0]
+    return jnp.concatenate([p[c : c + 8] for c in range(0, tall, 8) for p in parts], axis=0)
+
+
 fields = (
     "dest", "slot", "pos", "species", "feat", "halo", "wave", "nbr", "count", "rin", "mid",
     "rout", "up", "prod", "ow", "sw", "charge", "fieldw", "readw", "rvec", "fw",
@@ -73,12 +79,12 @@
     gx, yz, nyp = sizes
     n_in = len(fields)
     sources, refs = refs[:n_in], refs[n_in:]
-    forces, energies = refs[:2]
-    local, refs = dict(zip(fields, refs[2 : 2 + n_in])), refs[2 + n_in :]
+    out, refs = refs[0], refs[1:]
+    local, refs = dict(zip(fields, refs[:n_in])), refs[n_in:]
     (
         meta_in, meta_got, spread, pieces, work, halo_pos, ghost_pos, halo_feat, ghost_feat,
         xz, ymat, ypair, part_out, part_got, row_sum, row_got, coef, coefs,
-        rel, hidden, radials, table_t, acc, back, came,
+        rel, hidden, radials, hots, table_t, acc, back, came,
         in_s, meta_s, meta_r, sp_s, sp_r, pc_s, pc_r, hp_s, hp_r, hf_s, hf_r, rs_s, rs_r,
         gs_s, gs_r, ag_s, ag_r, ret_s, ret_r,
     ) = refs
@@ -191,7 +197,8 @@
     rin_t = jnp.concatenate([rin[...].astype(f32), jnp.zeros_like(rin, f32)], axis=0).T.astype(bf16)
     mid = use("mid")
     mid_t = [flip(mid[i]) for i in range(2)]
-    rout_t = flip(use("rout")[...])
+    tall = use("rout")[...].astype(f32).T
+    rout_t = interleave([tall[p * channels : (p + 1) * channels] for p in range(4)]).astype(bf16)
     list4 = jnp.concatenate([use("halo")[...]] * 4, axis=1)
     pick_t = (iota((atoms, 4 * halos), 0) == list4).astype(f32)
     pick = pick_t.T[:halos].astype(bf16)
@@ -200,6 +207,26 @@
     to_b = nt(force8, ow[1].astype(f32), highest)
     to_f = nt(force8, sw[1].astype(f32), highest)
     nbr, counts = use("nbr"), use("count")[...]
+
+    packed = 16
+    base = iota((packed, atoms), 0).astype(f32).astype(bf16)
+    one, nil = jnp.ones((packed, atoms), bf16), jnp.zeros((packed, atoms), bf16)
+
+    def hot_of(index):
+        near = jnp.broadcast_to(index, (packed, atoms)).astype(f32)
+        far = (near - atoms).astype(bf16)
+        near = near.astype(bf16)
+        tiles = [jnp.where(near - t == base, one, nil) for t in range(0, atoms, packed)]
+        tiles += [jnp.where(far - t == base, one, nil) for t in range(0, 4 * halos, packed)]
+        return jnp.concatenate(tiles, axis=0)
+
+    def hot_step(g, carry):
+        index = nbr[pl.ds(pl.multiple_of(g * group, group), group), :]
+        for s in range(group):
+            hots[g, s] = hot_of(index[s : s + 1])
+        return carry
+
+    lax.fori_loop(0, groups, hot_step, 0)
 
     arrive(meta_copies)
     metas = []
@@ -265,6 +292,14 @@
     table = table_pos.shape[1]
     nrad = rin.shape[0]
     centres = iota((2 * nrad, atoms), 0).astype(f32) * (cutoff_radius / (nrad - 1))
+
+    halfway = groups // 2
+
+    def emit(g, begin=0, end=group):
+        for s in range(begin, end):
+            radials[g, s] = mm(rout_t, hidden[g, s]).astype(bf16)
+
+    hidden[0] = jnp.zeros_like(hidden[0])
 
     def radial_step(g, carry):
         index = nbr[pl.ds(pl.multiple_of(g * group, group), group), :]
@@ -299,14 +334,18 @@
         for s in range(group):
             off = dist[s : s + 1] - centres
             basis.append(jnp.exp(-basis_sharpness * off * off))
-        h = silu(mm(rin_t, jnp.concatenate(basis, axis=1).astype(bf16))).astype(bf16)
-        h = silu(mm(mid_t[0], h)).astype(bf16)
-        h = silu(mm(mid_t[1], h))
+        h = mm(rin_t, jnp.concatenate(basis, axis=1).astype(bf16))
+        emit(g, 0, 2)
+        h = mm(mid_t[0], silu(h).astype(bf16))
+        emit(g, 2, 5)
+        h = mm(mid_t[1], silu(h).astype(bf16))
+        emit(g, 5, group)
+        h = silu(h)
         for s in range(group):
-            hidden[g, s] = (h[:, s * atoms : (s + 1) * atoms] * env[s : s + 1]).astype(bf16)
+            hidden[g + 1, s] = (h[:, s * atoms : (s + 1) * atoms] * env[s : s + 1]).astype(bf16)
         return carry
 
-    lax.fori_loop(0, groups, radial_step, 0)
+    lax.fori_loop(0, halfway, radial_step, 0)
 
     arrive(piece_copies)
     owned = work[...].reshape(atoms, width)
@@ -333,10 +372,10 @@
     up = use("up")
 
     def raise_rows(rows, begin, size):
-        for p in range(4):
-            cut = slice(p * channels, (p + 1) * channels)
-            got = mm(rows[:, cut], up[min(p, 1)])
-            table_t[cut, begin : begin + size] = got.T.astype(bf16)
+        parts = [
+            mm(rows[:, p * channels : (p + 1) * channels], up[min(p, 1)]).T for p in range(4)
+        ]
+        table_t[:, begin : begin + size] = interleave(parts).astype(bf16)
 
     raise_rows(owned, 0, atoms)
 
@@ -356,32 +395,34 @@
     stack = jnp.concatenate([high, blank, middle, blank, low, blank], axis=0)
     p_t = tn(stack.astype(bf16), jnp.concatenate([which] * 3, axis=0))
 
-    def spread_step(g, carry):
-        for s in range(group):
-            radials[g, s] = mm(rout_t, hidden[g, s]).astype(bf16)
-        return carry
-
-    lax.fori_loop(0, groups, spread_step, 0)
+    lax.fori_loop(halfway, groups, radial_step, 0)
+    emit(groups)
     acc[...] = jnp.zeros_like(acc)
     arrive(halo_copies)
     raise_rows(jnp.concatenate([ghost_feat[i] for i in range(4)], axis=0), atoms, 4 * halos)
 
     def message_step(g, carry):
-        index = nbr[pl.ds(pl.multiple_of(g * group, group), group), :]
-        r = [rel[g, m] for m in range(3)]
-        for s in range(group):
-            hot_t = (iota((table, atoms), 0) == index[s : s + 1]).astype(f32).astype(bf16)
-            u = mm(table_t[...], hot_t)
-            us = [u[p * channels : (p + 1) * channels] for p in range(4)]
-            rads = [
-                radials[g, s, p * channels : (p + 1) * channels, :].astype(f32) for p in range(4)
+        for begin in range(0, group, together):
+            chosen = range(begin, begin + together)
+            ups = [mm(table_t[...], hots[g, s]) for s in chosen]
+            rm = [
+                [jnp.broadcast_to(rel[g, m, s : s + 1, :], (8, atoms)) for m in range(3)]
+                for s in chosen
             ]
-            rm = [r[m][s : s + 1] for m in range(3)]
-            along = rm[0] * us[1] + rm[1] * us[2] + rm[2] * us[3]
-            acc[0] += rads[0] * us[0] + rads[1] * along
-            ru = rads[2] * us[0]
-            for m in range(3):
-                acc[1 + m] += ru * rm[m] + rads[3] * us[1 + m]
+            for c in range(channels // 8):
+                sums = [None] * 4
+                for i, s in enumerate(chosen):
+                    rows = ups[i][32 * c : 32 * c + 32]
+                    u = [rows[8 * p : 8 * p + 8] for p in range(4)]
+                    rows = radials[g + 1, s, 32 * c : 32 * c + 32, :].astype(f32)
+                    rad = [rows[8 * p : 8 * p + 8] for p in range(4)]
+                    x, y, z = rm[i]
+                    ru = rad[2] * u[0]
+                    terms = [rad[0] * u[0] + rad[1] * (x * u[1] + y * u[2] + z * u[3])]
+                    terms += [ru * rm[i][m] + rad[3] * u[1 + m] for m in range(3)]
+                    sums = [t if p is None else p + t for p, t in zip(sums, terms)]
+                for m in range(4):
+                    acc[c, m] += sums[m]
         return carry
 
     first, second = groups // 4, 5 * groups // 8
@@ -439,8 +480,8 @@
 
     scale = 1.0 / math.sqrt(slots)
     p = [p_t[i * channels : (i + 1) * channels] for i in range(5)]
-    a0 = acc[0] * scale
-    a1 = [acc[1 + m] * scale for m in range(3)]
+    a0 = acc[:, 0].reshape(channels, atoms) * scale
+    a1 = [acc[:, 1 + m].reshape(channels, atoms) * scale for m in range(3)]
     square = a1[0] * a1[0] + a1[1] * a1[1] + a1[2] * a1[2]
     b0 = (p[0] * a0 + p[1] * a0 * a0 + p[2] * square).astype(bf16)
     b1 = [(p[3] * a1[m] + p[4] * a0 * a1[m]).astype(bf16) for m in range(3)]
@@ -475,11 +516,15 @@
     total = back[0]
     for k in range(1, yz):
         total = total + came[k]
-    forces[...] = total[:3]
-    energies[...] = total[3:4]
+    out[...] = total
     for c in sent:
         c.wait_send()
     assert not loads
+
+
+def home_kernel(results, forces, energies):
+    forces[...] = results[:3]
+    energies[...] = results[3:4]
 
 
 def on_device(
@@ -569,28 +614,35 @@
         pltpu.VMEM((share, wide), f32),
         pltpu.VMEM((yz, share, wide), f32),
         pltpu.VMEM((groups, 3, group, atoms), f32),
-        pltpu.VMEM((groups, group, hidden, atoms), bf16),
-        pltpu.VMEM((groups, group, width, atoms), bf16),
+        pltpu.VMEM((groups + 1, group, hidden, atoms), bf16),
+        pltpu.VMEM((groups + 1, group, width, atoms), bf16),
+        pltpu.VMEM((groups, group, table, atoms), bf16),
         pltpu.VMEM((width, table), bf16),
-        pltpu.VMEM((4, channels, atoms), f32),
+        pltpu.VMEM((channels // 8, 4, 8, atoms), f32),
         pltpu.VMEM((yz, 8, atoms), f32),
         pltpu.VMEM((yz, 8, atoms), f32),
     ]
     scratch += [pltpu.SemaphoreType.DMA((len(fields),))]
     scratch += dma(yz) + dma(yz) + dma(yz) + dma(4) + dma(4) + dma(yz) + dma(gx) + dma(yz) + dma(yz)
-    forces, energies = pl.pallas_call(
+    results = pl.pallas_call(
         functools.partial(step_kernel, (gx, yz, nyp)),
-        out_shape=[
-            jax.ShapeDtypeStruct((3, atoms), f32),
-            jax.ShapeDtypeStruct((1, atoms), f32),
-        ],
+        out_shape=jax.ShapeDtypeStruct((8, atoms), f32),
         in_specs=[pl.BlockSpec(memory_space=pl.ANY)] * len(fields),
-        out_specs=[VMEM, VMEM],
+        out_specs=VMEM,
         scratch_shapes=scratch,
         compiler_params=pltpu.CompilerParams(
             collective_id=0, has_side_effects=True, vmem_limit_bytes=56 * 1024 * 1024
         ),
     )(*[given[name] for name in fields])
+    forces, energies = pl.pallas_call(
+        home_kernel,
+        out_shape=[
+            jax.ShapeDtypeStruct((3, atoms), f32),
+            jax.ShapeDtypeStruct((1, atoms), f32),
+        ],
+        in_specs=[VMEM],
+        out_specs=[VMEM, VMEM],
+    )(results)
     return forces, energies.reshape(atoms)
 
 

time: 50.4 us -> 44.7 us (0.89)
  Pallas kernels: 47.7 us -> 43.8 us
  local copies, waits for them, and re-layouts: 1.87 us -> 0 us
    pallas_call x1 -> x2, Pallas kernels: 47.7 us -> 43.8 us  [the longest x1 42.5 us: on_device(): pl.pallas_call(functools.partial(step_kernel, (gx, yz, nyp)), out_shape=j...]
    unnamed x6 -> x0, local copies, waits for them, and re-layouts: 1.87 us -> none
where the time goes in v3:
time: 44.7 us; the launch traced here: 44.5 us
  Pallas kernels  43.8 us (98%)
  between operations  0.65 us (1%)
    pallas_call x1, Pallas kernels, on_device(): pl.pallas_call(functools.partial(step_kernel, (gx, yz, nyp)), out_shape=j...  42.5 us
    pallas_call x1, Pallas kernels, on_device(): pl.pallas_call(home_kernel, out_shape=[jax.ShapeDtypeStruct((3, atoms), f...  1.29 us

profile of v3, /device:TPU:0, one launch (start us, length us, event | category | flops | bytes accessed | tf_op | source)
XLA Modules:
  0.0 44.5 jit_solution(1913360851508196819)
XLA Ops:
  0.6 42.5 %shard_map.212.results = f32[8,256]{1,0:T(8,128)} custom-call(s32[1,2]{1,0:T(1,128)} %bitcast.18, s32[1,2]{1,0:T(1,128)} %bitcast.19, bf16[3,256]{1,0:T(4,128)(2,1)} %refs_2_.1, s32[1,256]{1,0:T(1,128)} %bitcast.16, bf16[2,8,16,512]{3,2,1,0:T(8,128)(2,1)} %bitcast.12, s32[1,32]{1,0:T(1,128)} %bitcast.20, s32[3,4096]{1,0:T(4,128)} %refs_6_.1, ...), custom_call_target="tpu_custom_call" | custom-call | tf_op jit(solution)/shard_map/pallas_call | solution.py:627
  43.2 1.3 %shard_map.213 = (f32[3,256]{1,0:T(4,128)}, f32[1,256]{1,0:T(1,128)}) custom-call(f32[8,256]{1,0:T(8,128)} %shard_map.212.results), custom_call_target="tpu_custom_call" | custom-call | tf_op jit(solution)/shard_map/pallas_call | solution.py:637

commit v4 on v3

--- a/solution.py
+++ b/solution.py
@@ -282,6 +282,18 @@
     )
     work[:, pl.ds(me, 1)] = pieces[me].reshape(blocks, 1, piece, width)
 
+    prod = use("prod")
+    kinds = prod.shape[0]
+    which = (iota((8, atoms), 0).astype(f32) == meta[3:4]).astype(f32).astype(bf16)
+    weights = prod[...]
+    high = weights.astype(bf16).astype(f32)
+    middle = (weights - high).astype(bf16).astype(f32)
+    low = weights - high - middle
+    blank = jnp.zeros((8 - kinds, weights.shape[1]), f32)
+    stack = jnp.concatenate([high, blank, middle, blank, low, blank], axis=0)
+    p_t = tn(stack.astype(bf16), jnp.concatenate([which] * 3, axis=0))
+    acc[...] = jnp.zeros_like(acc)
+    hidden[0] = jnp.zeros_like(hidden[0])
     arrive(ghost_copies)
     part = iota((8, 4 * halos), 1) // halos
     lead = iota((8, 4 * halos), 0)
@@ -299,7 +311,6 @@
         for s in range(begin, end):
             radials[g, s] = mm(rout_t, hidden[g, s]).astype(bf16)
 
-    hidden[0] = jnp.zeros_like(hidden[0])
 
     def radial_step(g, carry):
         index = nbr[pl.ds(pl.multiple_of(g * group, group), group), :]
@@ -384,20 +395,9 @@
         nt(to_f, owned[:, (1 + m) * channels : (2 + m) * channels].astype(f32), highest)[0:1]
         for m in range(3)
     ]
-    prod = use("prod")
-    kinds = prod.shape[0]
-    which = (iota((8, atoms), 0).astype(f32) == meta[3:4]).astype(f32).astype(bf16)
-    weights = prod[...]
-    high = weights.astype(bf16).astype(f32)
-    middle = (weights - high).astype(bf16).astype(f32)
-    low = weights - high - middle
-    blank = jnp.zeros((8 - kinds, weights.shape[1]), f32)
-    stack = jnp.concatenate([high, blank, middle, blank, low, blank], axis=0)
-    p_t = tn(stack.astype(bf16), jnp.concatenate([which] * 3, axis=0))
 
     lax.fori_loop(halfway, groups, radial_step, 0)
     emit(groups)
-    acc[...] = jnp.zeros_like(acc)
     arrive(halo_copies)
     raise_rows(jnp.concatenate([ghost_feat[i] for i in range(4)], axis=0), atoms, 4 * halos)
 

time: 44.7 us -> 44.5 us (level)
  no operation moved by 1% of the time
where the time goes in v4:
time: 44.5 us; the launch traced here: 44.3 us
  Pallas kernels  43.6 us (98%)
  between operations  0.65 us (1%)
    pallas_call x1, Pallas kernels, on_device(): pl.pallas_call(functools.partial(step_kernel, (gx, yz, nyp)), out_shape=j...  42.3 us
    pallas_call x1, Pallas kernels, on_device(): pl.pallas_call(home_kernel, out_shape=[jax.ShapeDtypeStruct((3, atoms), f...  1.29 us

profile of v4, /device:TPU:0, one launch (start us, length us, event | category | flops | bytes accessed | tf_op | source)
XLA Modules:
  0.0 44.3 jit_solution(12899894437788183339)
XLA Ops:
  0.6 42.3 %shard_map.212.results = f32[8,256]{1,0:T(8,128)} custom-call(s32[1,2]{1,0:T(1,128)} %bitcast.18, s32[1,2]{1,0:T(1,128)} %bitcast.19, bf16[3,256]{1,0:T(4,128)(2,1)} %refs_2_.1, s32[1,256]{1,0:T(1,128)} %bitcast.16, bf16[2,8,16,512]{3,2,1,0:T(8,128)(2,1)} %bitcast.12, s32[1,32]{1,0:T(1,128)} %bitcast.20, s32[3,4096]{1,0:T(4,128)} %refs_6_.1, ...), custom_call_target="tpu_custom_call" | custom-call | tf_op jit(solution)/shard_map/pallas_call | solution.py:627
  43.0 1.3 %shard_map.213 = (f32[3,256]{1,0:T(4,128)}, f32[1,256]{1,0:T(1,128)}) custom-call(f32[8,256]{1,0:T(8,128)} %shard_map.212.results), custom_call_target="tpu_custom_call" | custom-call | tf_op jit(solution)/shard_map/pallas_call | solution.py:637
